TPU v7x, 32 devices: a whole 2x2x4 slice. The times are simulated.
32 devices in a mesh: gx: 4 (over z), gy: 2 (over y), gz: 4 (over x, core).
Axes of the slice: x: 2, y: 2, z: 4, core: 2. Of those that a mesh axis runs over, the one named last changes fastest.
Arguments:
- iterate: float32 [32, 32, 512], P('gx', 'gy', 'gz'), may hold values from -6 to 6
- source: float32 [32, 32, 512], P('gx', 'gy', 'gz'), may hold values from -6 to 6
- reaction: float32 [32, 32, 512], P('gx', 'gy', 'gz'), may hold values from 0.05 to 1
- trial_powers: int32 [4], replicated, may hold values from 0 to 5
Outputs:
- newton_dir: float32 [32, 32, 512], P('gx', 'gy', 'gz')
- remnant: float32 [32, 32, 512], P('gx', 'gy', 'gz')
- layer_energies: float32 [4, 32], P(None, 'gx')
- energies: float32 [4], replicated
Inputs may be any that keep to these rules, and one draw needn't show every extreme that they name: `trial_powers`: trial k takes the step length 2 to the power minus entry k.
All inputs are finite; a program needn't handle non-finite values.
Results may differ from a plain program's by a relative error of at most 0.0003.
Values sent between devices are 32-bit elements; how exact they have to be, the bound alone decides.
A program may use at most 128 MiB of HBM per device.

v0:
```python
import functools

import jax
import jax.numpy as jnp
from jax import lax
from jax.experimental import pallas as pl
from jax.experimental.pallas import tpu as pltpu
from jax.sharding import PartitionSpec as P

ITERS = 4
LEVELS = 4
TRIALS = 4
MID = 1.15
HALF = 0.85
SIGMA = MID / HALF
RHO0 = 1.0 / SIGMA
RHO1 = 1.0 / (2.0 * SIGMA - RHO0)
RHO2 = 1.0 / (2.0 * SIGMA - RHO1)
ROUND = 3
KEPT = ROUND
DG, INV, XM, XP, YM, YP, ZM, ZP, YB, ZB = range(10)
MESH = pl.DeviceIdType.MESH


class Grid:
    def __init__(self, Y, Z):
        self.Y, self.Z = Y, Z

    def rows_of(self, x):
        return lax.rem(lax.broadcasted_iota(jnp.int32, (x * self.Y, self.Z), 0), self.Y)

    def lanes_of(self, x):
        return lax.broadcasted_iota(jnp.int32, (x * self.Y, self.Z), 1)

    def pair_x(self, v):
        Y = self.Y
        x = v.shape[0] // Y
        return cat([v[2 * i * Y : (2 * i + 1) * Y] + v[(2 * i + 1) * Y : (2 * i + 2) * Y] for i in range(x // 2)])

    def pick_x(self, v, odd):
        Y = self.Y
        x = v.shape[0] // Y
        return cat([v[(2 * i + odd) * Y : (2 * i + odd + 1) * Y] for i in range(x // 2)])

    def bit(self, v, level, axis):
        at = self.rows_of(v.shape[0] // self.Y) if axis == 0 else self.lanes_of(v.shape[0] // self.Y)
        return lax.rem(at, 2 << level) < (1 << level)

    def pair(self, v, level, axis):
        step = 1 << level
        return v + jnp.where(self.bit(v, level, axis), roll(v, -step, axis), roll(v, step, axis))

    def pick(self, v, level, axis, odd):
        step = 1 << level
        low = self.bit(v, level, axis)
        if odd:
            return jnp.where(low, roll(v, -step, axis), v)
        return jnp.where(low, v, roll(v, step, axis))

    def restrict(self, v, level):
        return self.pair(self.pair(self.pair_x(v), level, 0), level, 1)

    def prolong(self, v):
        Y = self.Y
        x = v.shape[0] // Y
        return cat([v[(i // 2) * Y : (i // 2 + 1) * Y] for i in range(2 * x)])

    def coarsen(self, ws, reaction, level):
        xm, xp, ym, yp, zm, zp = ws
        pair, pick = self.pair, self.pick
        ws = (
            pair(pair(self.pick_x(xm, 0), level, 0), level, 1),
            pair(pair(self.pick_x(xp, 1), level, 0), level, 1),
            pair(pick(self.pair_x(ym), level, 0, 0), level, 1),
            pair(pick(self.pair_x(yp), level, 0, 1), level, 1),
            pick(pair(self.pair_x(zm), level, 0), level, 1, 0),
            pick(pair(self.pair_x(zp), level, 0), level, 1, 1),
        )
        return ws, self.restrict(reaction, level)

    def put(self, w, level, ws, reaction):
        Y, Z = self.Y, self.Z
        xm, xp, ym, yp, zm, zp = ws
        step = 1 << level
        x = xm.shape[0] // Y
        rows, lanes = self.rows_of(x), self.lanes_of(x)
        diagonal = reaction + xm + xp + ym + yp + zm + zp
        zero = jnp.zeros_like(xm)
        w[DG] = diagonal
        w[INV] = 1.0 / diagonal
        w[XM] = xm
        w[XP] = xp
        w[YM] = jnp.where(rows < step, zero, ym)
        w[YP] = jnp.where(rows >= Y - step, zero, yp)
        w[ZM] = jnp.where(lanes < step, zero, zm)
        w[ZP] = jnp.where(lanes >= Z - step, zero, zp)
        if w.shape[0] > YB:
            w[YB] = jnp.where(rows < step, ym, jnp.where(rows >= Y - step, yp, zero))
            w[ZB] = jnp.where(lanes < step, zm, jnp.where(lanes >= Z - step, zp, zero))

    def inner(self, w, v, level):
        step = 1 << level
        acc = w[DG] * v
        acc = acc - w[YM] * roll(v, step, 0) - w[YP] * roll(v, -step, 0)
        acc = acc - w[ZM] * roll(v, step, 1) - w[ZP] * roll(v, -step, 1)
        Y = self.Y
        if v.shape[0] > Y:
            none = jnp.zeros((Y, self.Z), jnp.float32)
            acc = acc - w[XM] * cat([none, v[:-Y]]) - w[XP] * cat([v[Y:], none])
        return acc


def cat(parts):
    return parts[0] if len(parts) == 1 else jnp.concatenate(parts, axis=0)


def roll(v, shift, axis):
    return pltpu.roll(v, shift % v.shape[axis], axis)


def dot(a, b):
    return lax.dot_general(
        a, b, (((1,), (0,)), ((), ())), precision=lax.Precision.HIGHEST, preferred_element_type=jnp.float32
    )


def kernel(
    sizes, counts, tp_ref, it_ref, src_ref, rea_ref, dir_ref, rem_ref, le_ref, en_ref,
    sx, rx, sy, ry, sz, rz, ssem, rsem, lev0, lev1, glev2, glev3, p_ref, q_ref,
    phx, phy, phz, dhx, dhy, dhz, dot_all, en_all, red_ssem, red_rsem,
    picked, gat_pl, gat_x, set_pl, set_x, glob,
):
    X, Y, Z = sizes
    nx, ny, nz = counts
    planes = ny * nz
    levs = (lev0, lev1)
    L = len(levs)
    x_own, y_own, z_own = X >> L, Y >> L, Z >> L
    GY, GZ = ny * y_own, nz * z_own
    here, world = Grid(Y, Z), Grid(GY, GZ)
    rows_of, lanes_of = here.rows_of, here.lanes_of
    ix, iy, iz = lax.axis_index("gx"), lax.axis_index("gy"), lax.axis_index("gz")
    has = (ix > 0, ix < nx - 1, iy > 0, iy < ny - 1, iz > 0, iz < nz - 1)
    devs = (
        (ix - 1, iy, iz), (ix + 1, iy, iz), (ix, iy - 1, iz),
        (ix, iy + 1, iz), (ix, iy, iz - 1), (ix, iy, iz + 1),
    )
    send = (sx, sx, sy, sy, sz, sz)
    recv = (rx, rx, ry, ry, rz, rz)
    lane_y = lax.broadcasted_iota(jnp.int32, (Y, Z), 1)
    lane_1 = lax.broadcasted_iota(jnp.int32, (1, Z), 1)

    for d in range(6):
        @pl.when(jnp.logical_not(has[d]))
        def _():
            recv[d][:, d % 2] = jnp.zeros(recv[d].shape[:1] + recv[d].shape[2:], jnp.float32)

    def outgoing(d, slot):
        side = d % 2
        return pltpu.make_async_remote_copy(
            src_ref=send[d].at[slot, side],
            dst_ref=recv[d].at[slot, 1 - side],
            send_sem=ssem.at[slot, d],
            recv_sem=rsem.at[slot, d + 1 - 2 * side],
            device_id=devs[d],
            device_id_type=MESH,
        )

    def incoming(d, slot):
        side = d % 2
        return pltpu.make_async_remote_copy(
            src_ref=send[d].at[slot, side],
            dst_ref=recv[d].at[slot, side],
            send_sem=ssem.at[slot, d],
            recv_sem=rsem.at[slot, d],
            device_id=devs[d],
            device_id_type=MESH,
        )

    def go(d, slot):
        @pl.when(has[d])
        def _():
            outgoing(d, slot).start()

    def start(v, slot):
        x = v.shape[0] // Y
        sx[slot, 0] = v[:Y]
        sx[slot, 1] = v[-Y:]
        go(0, slot)
        go(1, slot)
        for i in range(x):
            sy[slot, 0, i : i + 1] = v[i * Y : i * Y + 1]
            sy[slot, 1, i : i + 1] = v[i * Y + Y - 1 : i * Y + Y]
        go(2, slot)
        go(3, slot)
        for side, lane in ((0, 0), (1, Z - 1)):
            packed = jnp.broadcast_to(v[:Y, lane : lane + 1], (Y, Z))
            for i in range(1, x):
                part = jnp.broadcast_to(v[i * Y : i * Y + Y, lane : lane + 1], (Y, Z))
                packed = jnp.where(lane_y == i, part, packed)
            sz[slot, side] = packed
        go(4, slot)
        go(5, slot)

    def finish(slot):
        for d in range(6):
            @pl.when(has[d])
            def _():
                copy = incoming(d, slot)
                copy.wait_recv()
                copy.wait_send()

    def wide_y(half, x):
        return cat([jnp.broadcast_to(half[i : i + 1], (Y, Z)) for i in range(x)])

    def wide_z(half, x):
        return cat([jnp.broadcast_to(half[:, i : i + 1], (Y, Z)) for i in range(x)])

    def beyond(w, acc, in_x0, in_x1, in_y, in_z):
        x = acc.shape[0] // Y
        acc = acc - w[YB] * in_y - w[ZB] * in_z
        low = w[XM, :Y] * in_x0
        high = w[XP, (x - 1) * Y :] * in_x1
        if x == 1:
            return acc - low - high
        return cat([acc[:Y] - low] + ([acc[Y:-Y]] if x > 2 else []) + [acc[-Y:] - high])

    def operate(v, level, slot):
        w = levs[level]
        x = X >> level
        start(v, slot)
        acc = here.inner(w, v, level)
        finish(slot)
        in_y = jnp.where(rows_of(x) < Y // 2, wide_y(ry[slot, 0], x), wide_y(ry[slot, 1], x))
        in_z = jnp.where(lanes_of(x) < Z // 2, wide_z(rz[slot, 0], x), wide_z(rz[slot, 1], x))
        return beyond(w, acc, rx[slot, 0], rx[slot, 1], in_y, in_z)

    turn = [0]

    def apply(v, level):
        slot = turn[0] % ROUND
        turn[0] += 1
        return operate(v, level, slot)

    def vcycle(r, level, part):
        w = levs[level]
        u = w[INV] * r * (1.0 / MID)
        total = u
        r = r - apply(u, level)
        u = RHO1 * RHO0 * u + 2.0 * RHO1 / HALF * w[INV] * r
        total = total + u
        r = r - apply(u, level)
        coarse = here.restrict(r, level)
        if level + 1 < L:
            e = here.prolong(vcycle(coarse, level + 1, part))
            r = r - apply(e, level)
        else:
            everywhere = collect(coarse, 1, part, gat_pl, gat_x, 4)
            e, ends = spread(world_cycle(everywhere[0], level + 1))
            r = r - beyond(w, here.inner(w, e, level), *ends)
        total = total + e
        u = w[INV] * r * (1.0 / MID)
        total = total + u
        r = r - apply(u, level)
        u = RHO1 * RHO0 * u + 2.0 * RHO1 / HALF * w[INV] * r
        return total + u

    def world_cycle(r, level):
        w = (glev2, glev3)[level - L]

        def apply(v):
            return world.inner(w, v, level - L)

        u = w[INV] * r * (1.0 / MID)
        total = u
        r = r - apply(u)
        u = RHO1 * RHO0 * u + 2.0 * RHO1 / HALF * w[INV] * r
        total = total + u
        r = r - apply(u)
        if level == LEVELS - 1:
            u = RHO2 * RHO1 * u + 2.0 * RHO2 / HALF * w[INV] * r
            return total + u
        e = world.prolong(world_cycle(world.restrict(r, level - L), level + 1))
        total = total + e
        r = r - apply(e)
        u = w[INV] * r * (1.0 / MID)
        total = total + u
        r = r - apply(u)
        u = RHO1 * RHO0 * u + 2.0 * RHO1 / HALF * w[INV] * r
        return total + u

    def hot(shape, wanted):
        at = lax.broadcasted_iota(jnp.int32, shape, 0)
        return jnp.where(at == wanted, 1.0, 0.0)

    def collect(v, fields, part, pl_ref, x_ref, which):
        count = fields * x_own * y_own
        picked[: fields * x_own * Y] = v
        own = picked[pl.ds(0, count, stride=1 << L), :]
        lane = lax.broadcasted_iota(jnp.int32, (Z, GZ), 1) - iz * z_own
        inside = jnp.logical_and(lane >= 0, lane < z_own)
        put = hot((Z, GZ), jnp.where(inside, lane * (1 << L), -1))
        pl_ref[part, my_plane] = dot(own, put)
        gather(pl_ref, part, planes, my_plane, in_plane, which)
        for j in range(ny):
            rows = pl_ref[part, j * nz]
            for k in range(1, nz):
                rows = rows + pl_ref[part, j * nz + k]
            for i in range(fields * x_own):
                x_ref[part, ix, i * GY + j * y_own : i * GY + (j + 1) * y_own] = rows[i * y_own : (i + 1) * y_own]
        gather(x_ref, part, nx, ix, in_column, which + 1)
        return [
            cat([x_ref[part, d, f * x_own * GY : (f + 1) * x_own * GY] for d in range(nx)]) for f in range(fields)
        ]

    def spread(v):
        lane = lax.broadcasted_iota(jnp.int32, (GZ, Z), 1)
        inside = hot((GZ, Z), iz * z_own + lane // (1 << L))
        outside = hot((GZ, Z), jnp.where(lane < Z // 2, iz * z_own - 1, iz * z_own + z_own))
        glob[0, GY : GY + nx * x_own * GY] = dot(v, inside)
        glob[1, GY : GY + nx * x_own * GY] = dot(v, outside)
        rows = rows_of(1)

        def layer(which, a):
            base = (ix * x_own + 1 + a) * GY + iy * y_own
            out = jnp.broadcast_to(glob[which, pl.ds(base, 1), :], (Y, Z))
            for j in range(1, y_own):
                row = jnp.broadcast_to(glob[which, pl.ds(base + j, 1), :], (Y, Z))
                out = jnp.where(rows < j << L, out, row)
            return out

        def rims(a):
            base = (ix * x_own + 1 + a) * GY + iy * y_own
            low = glob[0, pl.ds(base - 1, 1), :] * has_low
            high = glob[0, pl.ds(base + y_own, 1), :] * has_high
            return jnp.where(rows < Y // 2, jnp.broadcast_to(low, (Y, Z)), jnp.broadcast_to(high, (Y, Z)))

        has_low = jnp.where(iy > 0, 1.0, 0.0)
        has_high = jnp.where(iy < ny - 1, 1.0, 0.0)
        own = range(x_own)
        e = here.prolong(cat([layer(0, a) for a in own]))
        in_y = here.prolong(cat([rims(a) for a in own]))
        in_z = here.prolong(cat([layer(1, a) for a in own]))
        return e, (layer(0, -1), layer(0, x_own), in_y, in_z)

    def gather(ref, part, count, me, device, which):
        for j in range(count):
            @pl.when(me != j)
            def _():
                pltpu.make_async_remote_copy(
                    src_ref=ref.at[part, me],
                    dst_ref=ref.at[part, me],
                    send_sem=red_ssem.at[which, part],
                    recv_sem=red_rsem.at[which, part],
                    device_id=device(j),
                    device_id_type=MESH,
                ).start()
        if count > 1:
            others = ref.at[part, pl.ds(0, count - 1)]
            pltpu.make_async_copy(others, others, red_rsem.at[which, part]).wait()
            pltpu.make_async_copy(others, others, red_ssem.at[which, part]).wait()

    def in_plane(j):
        return (ix, j // nz, j % nz)

    def in_column(j):
        return (j, iy, iz)

    def in_grid(j):
        return (j // planes, j // nz % ny, j % nz)

    my_plane = iy * nz + iz
    me = ix * planes + my_plane

    def reduce_plane(ref, part, value, which):
        ref[part, my_plane] = value
        gather(ref, part, planes, my_plane, in_plane, which)
        return jnp.sum(ref[part], axis=0)

    def reduce_column(ref, part, value, which):
        ref[part, ix] = value
        gather(ref, part, nx, ix, in_column, which)
        return jnp.sum(ref[part], axis=0)

    def total_of(v):
        return jnp.sum(jnp.sum(v, axis=0, keepdims=True), axis=1, keepdims=True)

    def lane_of(row, i):
        return jnp.sum(jnp.where(lane_1 == i, row, 0.0), axis=1, keepdims=True)

    it = it_ref[...].reshape(X * Y, Z)
    reaction = rea_ref[...].reshape(X * Y, Z)
    start(it, KEPT)
    finish(KEPT)
    rows, lanes = rows_of(X), lanes_of(X)
    last_row, last_lane = rows == Y - 1, lanes == Z - 1
    n_xm = cat([rx[KEPT, 0], it[:-Y]])
    n_xp = cat([it[Y:], rx[KEPT, 1]])
    n_ym = jnp.where(rows == 0, wide_y(ry[KEPT, 0], X), roll(it, 1, 0))
    n_yp = jnp.where(last_row, wide_y(ry[KEPT, 1], X), roll(it, -1, 0))
    n_zm = jnp.where(lanes == 0, wide_z(rz[KEPT, 0], X), roll(it, 1, 1))
    n_zp = jnp.where(last_lane, wide_z(rz[KEPT, 1], X), roll(it, -1, 1))
    ws = []
    r = src_ref[...].reshape(X * Y, Z) - reaction * it
    for sign, n in ((-1, n_xm), (1, n_xp), (-1, n_ym), (1, n_yp), (-1, n_zm), (1, n_zp)):
        g = n - it
        square = g * g
        root = jnp.sqrt(1.0 + square)
        ws.append((1.0 + 2.0 * square) / root)
        r = r + g * root
    rem_ref[...] = r.reshape(X, Y, Z)
    here.put(levs[0], 0, ws, reaction)
    for level in range(L):
        ws, reaction = here.coarsen(ws, reaction, level)
        if level + 1 < L:
            here.put(levs[level + 1], level + 1, ws, reaction)
    glob[...] = jnp.zeros_like(glob)
    *ws, reaction = collect(cat(list(ws) + [reaction]), 7, 0, set_pl, set_x, 6)
    world.put(glev2, 0, ws, reaction)
    world.put(glev3, 1, *world.coarsen(ws, reaction, 0))
    for ref in (p_ref, q_ref, phx, phy, phz, dhx, dhy, dhz):
        ref[...] = jnp.zeros_like(ref)
    dir_ref[...] = jnp.zeros_like(dir_ref)

    def body(it_idx, carry):
        rz_old, pq_old = carry
        part = lax.rem(it_idx, 2)
        r = rem_ref[...].reshape(X * Y, Z)
        turn[0] = 0
        z = vcycle(r, 0, part)
        z_slot = turn[0] % ROUND
        az = apply(z, 0)
        q_old = q_ref[...]
        sums = jnp.where(
            lane_1 == 0,
            total_of(rem_ref[...].reshape(X * Y, Z) * z),
            jnp.where(lane_1 == 1, total_of(z * az), total_of(z * q_old)),
        )
        dot_all[part, me] = sums
        gather(dot_all, part, nx * planes, me, in_grid, 0)
        row = jnp.sum(dot_all[part], axis=0)
        rz_new, zaz, zq = lane_of(row, 0), lane_of(row, 1), lane_of(row, 2)
        beta = rz_new / rz_old
        pq = zaz + 2.0 * beta * zq + beta * beta * pq_old
        a = rz_new / pq
        p = z + beta * p_ref[...]
        q = az + beta * q_old
        p_ref[...] = p
        q_ref[...] = q
        dir_ref[...] = dir_ref[...] + (a * p).reshape(X, Y, Z)
        rem_ref[...] = rem_ref[...] - (a * q).reshape(X, Y, Z)
        for got, ph, dh in ((rx, phx, dhx), (ry, phy, dhy), (rz, phz, dhz)):
            for side in range(2):
                edge = got[z_slot, side] + beta * ph[side]
                ph[side] = edge
                dh[side] = dh[side] + a * edge
        return rz_new, pq

    one = jnp.ones((1, 1), jnp.float32)
    lax.fori_loop(0, ITERS, body, (one, jnp.zeros((1, 1), jnp.float32)))

    it = it_ref[...].reshape(X * Y, Z)
    step_dir = dir_ref[...].reshape(X * Y, Z)

    def energy(g):
        square = 1.0 + g * g
        return (square * jnp.sqrt(square) - 1.0) * (1.0 / 3.0)

    ends_y = jnp.where(jnp.logical_and(last_row, iy == ny - 1), 1.0, 0.0)
    ends_z = jnp.where(jnp.logical_and(last_lane, iz == nz - 1), 1.0, 0.0)
    ends_x = jnp.where(ix == nx - 1, 1.0, 0.0)
    across = lax.broadcasted_iota(jnp.int32, (X, Z), 0) == lax.broadcasted_iota(jnp.int32, (X, Z), 1)
    trial_rows = []
    for k in range(TRIALS):
        s = jnp.exp2(-jnp.full((1, Z), tp_ref[k], jnp.int32).astype(jnp.float32))
        v = it + s * step_dir
        low_x = cat([rx[KEPT, 0] + s * dhx[0], v[:-Y]])
        low_y = jnp.where(rows == 0, wide_y(ry[KEPT, 0] + s * dhy[0], X), roll(v, 1, 0))
        low_z = jnp.where(lanes == 0, wide_z(rz[KEPT, 0] + s * dhz[0], X), roll(v, 1, 1))
        at_end = energy(v)
        e = energy(v - low_x) + energy(v - low_y) + energy(v - low_z)
        e = e + at_end * (ends_y + ends_z)
        e = cat([e[:-Y], e[-Y:] + ends_x * at_end[-Y:]]) if X > 1 else e + ends_x * at_end
        e = e + 0.5 * rea_ref[...].reshape(X * Y, Z) * v * v - src_ref[...].reshape(X * Y, Z) * v
        by_layer = jnp.sum(jnp.sum(e.reshape(X, Y, Z), axis=1), axis=1, keepdims=True)
        trial_rows.append(jnp.sum(jnp.where(across, by_layer, 0.0), axis=0, keepdims=True))
    en_all[0, me] = jnp.concatenate(trial_rows, axis=0)
    gather(en_all, 0, nx * planes, me, in_grid, 2)
    layers = jnp.sum(en_all[0, pl.ds(ix * planes, planes)], axis=0)
    layers = layers / (Y * ny * Z * nz)
    le_ref[...] = layers[:, :X]
    overall = jnp.sum(en_all[0], axis=0) / (Y * ny * Z * nz)
    overall = jnp.sum(overall, axis=1, keepdims=True) / (X * nx)
    en_ref[...] = jnp.broadcast_to(overall, (TRIALS, Z))


def on_device(counts, iterate, source, reaction, trial_powers):
    X, Y, Z = iterate.shape
    nx, ny, nz = counts
    f32 = jnp.float32
    slots = ROUND + 1
    vm = pltpu.VMEM
    scratch = [vm((slots, 2, rows, Z), f32) for rows in (Y, Y, X, X, Y, Y)]
    scratch += [pltpu.SemaphoreType.DMA((slots, 6))] * 2
    x_own, y_own = X // 4, Y // 4
    GX, GY, GZ = nx * x_own, ny * y_own, nz * Z // 4
    scratch += [vm((10, (X >> level) * Y, Z), f32) for level in range(2)]
    scratch += [vm((8, (GX >> level) * GY, GZ), f32) for level in range(2)]
    scratch += [vm((X * Y, Z), f32)] * 2
    scratch += [vm((2, rows, Z), f32) for rows in (Y, X, Y)] * 2
    scratch += [
        vm((2, nx * ny * nz, 1, Z), f32),
        vm((1, nx * ny * nz, TRIALS, Z), f32),
        pltpu.SemaphoreType.DMA((8, 2)), pltpu.SemaphoreType.DMA((8, 2)),
        vm((7 * x_own * Y, Z), f32),
        vm((2, ny * nz, x_own * y_own, GZ), f32), vm((2, nx, x_own * GY, GZ), f32),
        vm((1, ny * nz, 7 * x_own * y_own, GZ), f32), vm((1, nx, 7 * x_own * GY, GZ), f32),
        vm((2, (GX + 2) * GY, Z), f32),
    ]
    whole = pl.BlockSpec(memory_space=pltpu.VMEM)
    out = pl.pallas_call(
        functools.partial(kernel, (X, Y, Z), counts),
        out_shape=[
            jax.ShapeDtypeStruct((X, Y, Z), f32),
            jax.ShapeDtypeStruct((X, Y, Z), f32),
            jax.ShapeDtypeStruct((TRIALS, X), f32),
            jax.ShapeDtypeStruct((TRIALS, Z), f32),
        ],
        in_specs=[pl.BlockSpec(memory_space=pltpu.SMEM), whole, whole, whole],
        out_specs=[whole] * 4,
        scratch_shapes=scratch,
        compiler_params=pltpu.CompilerParams(has_side_effects=True, vmem_limit_bytes=48 * 1024 * 1024),
        name="newton_step",
    )(trial_powers, iterate, source, reaction)
    return out[0], out[1], out[2], out[3][:, 0]


def solution(mesh):
    counts = tuple(mesh.shape[axis] for axis in ("gx", "gy", "gz"))
    grid = P("gx", "gy", "gz")
    return jax.shard_map(
        functools.partial(on_device, counts),
        mesh=mesh,
        in_specs=(grid, grid, grid, P()),
        out_specs=(grid, grid, P(None, "gx"), P()),
        check_vma=False,
    )
```

profile of v0, /device:TPU:0, one launch (start us, length us, event | category | flops | bytes accessed | tf_op | source)
XLA Modules:
  0.0 175.9 jit_solution(5050277093254199309)
XLA Ops:
  0.6 0.0 copy-start
  0.6 0.8 copy-done
  1.5 0.0 copy-start.1
  1.5 0.8 copy-done.1
  2.3 0.0 copy-start.2
  2.3 0.8 copy-done.2
  3.2 0.0 copy-start.3
  3.2 0.7 copy-done.3
  3.8 169.6 %newton_step.1 = (f32[8,16,128]{2,1,0:T(8,128)S(1)}, f32[8,16,128]{2,1,0:T(8,128)S(1)}, f32[4,8]{1,0:T(4,128)S(1)}, f32[4,128]{1,0:T(4,128)S(1)}) custom-call(s32[4]{0:T(128)S(1)} %copy-done.3, f32[8,16,128]{2,1,0:T(8,128)S(1)} %copy-done, f32[8,16,128]{2,1,0:T(8,128)S(1)} %copy-done.1, f32[8,16,128]{2,1,0:T(8,128)S(1)} %copy-done.2), custom_call_target="tpu_custom_call" | custom-call | tf_op jit(solution)/shard_map/newton_step/pallas_call | solution.py:521
  173.4 0.6 slice_reduce_fusion
  174.1 0.6 copy.11
  174.7 0.6 copy.12
  175.3 0.6 copy.13
Async XLA Ops:
  0.6 0.8 copy-start
  1.5 0.8 copy-start.1
  2.3 0.8 copy-start.2
  3.2 0.7 copy-start.3
where the time goes:
time: 176 us
  Pallas kernels  170 us (97%)
  local copies, waits for them, and re-layouts  5.63 us (3%)
    pallas_call x1, Pallas kernels, on_device(): pl.pallas_call(functools.partial(kernel, (X, Y, Z), counts), out_shape=[j...  170 us
    unnamed x11, local copies, waits for them, and re-layouts  5 us

commit v1 on v0

--- a/solution.py
+++ b/solution.py
@@ -535,11 +535,791 @@
     return out[0], out[1], out[2], out[3][:, 0]
 
 
+LANES = 128
+HALO = 8
+F_DG, F_XM, F_YM, F_ZM, F_XP, F_YP, F_ZP, F_INV = range(8)
+C_ONE = RHO1 * RHO0
+C_TWO = 2.0 * RHO1 / HALF
+C_THREE = RHO2 * RHO1
+C_FOUR = 2.0 * RHO2 / HALF
+
+
+def slab_fits(counts, shape):
+    X, Y, Z = shape
+    nx, ny, _ = counts
+    return X == 1 << (LEVELS - 1) and X * Y == LANES and nx * ny == X and Z == 2 * HALO * X
+
+
+def slab_kernel(
+    sizes, counts, tp_ref, it_in, src_in, rea_in, dir_out, rem_out, le_ref, en_ref,
+    turned, d_it, d_rea, d_src, f_it, f_rea, f_src, w0, w1, w2, w3,
+    va, vb, vc, vd, vz, rr, rs, az, sa, ra, sb, rb, s0, r0, sq, rq,
+    ua, ub, uc, ud, r1in, r1by, rr1, rs1, sa1, ra1, sb1, rb1, s1, r1, sq1, rq1, e2, cres, cq,
+    p_ref, dir_ref, q_ref, r_ref,
+    msg, gath, rows_of, wmsg, wgath, hb, sh, emsg, egath, outs, back,
+    d_ssem, d_rsem, g_ssem, g_rsem, h_ssem, h_rsem,
+):
+    X, Y, Z = sizes
+    nx, ny, nz = counts
+    P = nx * ny
+    S = Z // P
+    GY = ny * Y
+    NS = nz * P
+    NZ = nz * Z
+    W = S + 2 * HALO
+    f32 = jnp.float32
+    ix, iy, iz = lax.axis_index("gx"), lax.axis_index("gy"), lax.axis_index("gz")
+    odd_z = lax.rem(iz, 2)
+    odd_y = lax.rem(iy, 2)
+    along = iy * nx + ix + odd_y * (nx - 1 - 2 * ix)
+    j = along + odd_z * (P - 1 - 2 * along)
+    slab = iz * P + j
+    me = (ix * ny + iy) * nz + iz
+    own_tile = ix * ny + iy
+
+    def device_at(jj, kz):
+        a = jj + lax.rem(kz, 2) * (P - 1 - 2 * jj)
+        y = a // nx
+        i = lax.rem(a, nx)
+        return (i + lax.rem(y, 2) * (nx - 1 - 2 * i), y, kz)
+
+    def device_of(s):
+        return device_at(lax.rem(s, P), s // P)
+
+    has_lo, has_hi = slab > 0, slab < NS - 1
+    lo_dev, hi_dev = device_of(jnp.maximum(slab - 1, 0)), device_of(jnp.minimum(slab + 1, NS - 1))
+
+    def lane(n):
+        return lax.broadcasted_iota(jnp.int32, (n, LANES), 1)
+
+    def row(n):
+        return lax.broadcasted_iota(jnp.int32, (n, LANES), 0)
+
+    def low_bit(n, step):
+        return lax.rem(lane(n), 2 * step) < step
+
+    def swap(v, step):
+        return jnp.where(low_bit(v.shape[0], step), roll(v, -step, 1), roll(v, step, 1))
+
+    def pair(v, step):
+        return v + swap(v, step)
+
+    def pick_low(v, step):
+        return jnp.where(low_bit(v.shape[0], step), v, roll(v, step, 1))
+
+    def pick_high(v, step):
+        return jnp.where(low_bit(v.shape[0], step), roll(v, -step, 1), v)
+
+    def block_transpose(tiles):
+        n = tiles[0].shape[0]
+        k = P // 2
+        while k:
+            low = low_bit(n, Y * k)
+            new = list(tiles)
+            for i in range(P):
+                if not i & k:
+                    a, b = tiles[i], tiles[i | k]
+                    new[i] = jnp.where(low, a, roll(b, Y * k, 1))
+                    new[i | k] = jnp.where(low, roll(a, -Y * k, 1), b)
+            tiles = new
+            k //= 2
+        return tiles
+
+    arrays = ((it_in, d_it, f_it, 2 * HALO), (rea_in, d_rea, f_rea, HALO), (src_in, d_src, f_src, HALO))
+    LOW, MID_PART, HIGH = range(3)
+
+    def piece(a, kind, src_row, count, dst_row, jd, kz):
+        return pltpu.make_async_remote_copy(
+            src_ref=turned.at[a, pl.ds(src_row, count)],
+            dst_ref=arrays[a][1].at[own_tile, pl.ds(dst_row, count)],
+            send_sem=d_ssem.at[a, kind, jd],
+            recv_sem=d_rsem.at[a, kind],
+            device_id=device_at(jd, kz),
+            device_id_type=MESH,
+        )
+
+    def pieces(a):
+        halo = arrays[a][3]
+        for jd in range(P):
+            yield j != jd, piece(a, MID_PART, S * jd, S, halo, jd, iz)
+            if jd > 0:
+                yield j != jd, piece(a, LOW, S * jd - halo, halo, 0, jd, iz)
+            else:
+                yield iz < nz - 1, piece(a, LOW, Z - halo, halo, 0, jd, iz + 1)
+            if jd < P - 1:
+                yield j != jd, piece(a, HIGH, S * jd + S, halo, halo + S, jd, iz)
+            else:
+                yield iz > 0, piece(a, HIGH, 0, halo, halo + S, jd, iz - 1)
+
+    for ref in (va, vb, vc, vd, vz, ua, ub, uc, ud, r1in, r1by, e2, hb, sh, p_ref, dir_ref, q_ref, sq, rq, sq1, rq1, cq, w1):
+        ref[...] = jnp.zeros_like(ref)
+    w1[F_DG] = jnp.ones(w1.shape[1:], f32)
+
+    for a, (given, landed, _, halo) in enumerate(arrays):
+        turned[a] = given[...].reshape(LANES, Z).T
+        for wanted, copy in pieces(a):
+            @pl.when(wanted)
+            def _():
+                copy.start()
+        landed[own_tile, halo : halo + S] = turned[a, pl.ds(pl.multiple_of(S * j, HALO), S)]
+
+        @pl.when(j > 0)
+        def _():
+            landed[own_tile, :halo] = turned[a, pl.ds(pl.multiple_of(S * j - halo, HALO), halo)]
+
+        @pl.when(j < P - 1)
+        def _():
+            landed[own_tile, halo + S :] = turned[a, pl.ds(pl.multiple_of(S * j + S, HALO), halo)]
+
+        @pl.when(slab == 0)
+        def _():
+            landed[:, :halo] = jnp.zeros((P, halo, LANES), f32)
+
+        @pl.when(slab == NS - 1)
+        def _():
+            landed[:, halo + S :] = jnp.zeros((P, halo, LANES), f32)
+
+    def landed_wait(a, kind, first, count, tiles):
+        view = arrays[a][1].at[pl.ds(0, tiles), pl.ds(first, count)]
+        pltpu.make_async_copy(view, view, d_rsem.at[a, kind]).wait()
+
+    for a, (_, landed, flat, halo) in enumerate(arrays):
+        landed_wait(a, MID_PART, halo, S, P - 1)
+        for kind, first, inner, outer in (
+            (LOW, 0, j > 0, jnp.logical_and(j == 0, iz > 0)),
+            (HIGH, halo + S, j < P - 1, jnp.logical_and(j == P - 1, iz < nz - 1)),
+        ):
+            @pl.when(inner)
+            def _():
+                landed_wait(a, kind, first, halo, P - 1)
+
+            @pl.when(outer)
+            def _():
+                landed_wait(a, kind, first, halo, P)
+        for at in range(0, S + 2 * halo, HALO):
+            tiles = block_transpose([landed[i, at : at + HALO] for i in range(P)])
+            for i in range(P):
+                flat[i, at : at + HALO] = tiles[i]
+
+    lanes = lane(W)
+    z_at = slab * S + row(W) - HALO
+    inside = jnp.logical_and(z_at >= 0, z_at < NZ)
+    z_low = jnp.logical_and(z_at > 0, z_at < NZ)
+    z_high = jnp.logical_and(z_at >= 0, z_at < NZ - 1)
+    x_first, x_last = lanes < GY, lanes >= LANES - GY
+    y_at = lax.rem(lanes, GY)
+    y_first, y_last = y_at == 0, y_at == GY - 1
+
+    def face(g):
+        square = g * g
+        root = jnp.sqrt(1.0 + square)
+        return (1.0 + 2.0 * square) / root, g * root
+
+    def window(t):
+        return f_it[t, HALO : HALO + W]
+
+    low_w, low_p = face(window(0) - jnp.where(x_first, 0.0, roll(window(X - 1), GY, 1)))
+    first_w = low_w
+    for t in range(X):
+        c = window(t)
+        beyond = window(t + 1) if t < X - 1 else jnp.where(x_last, 0.0, roll(window(0), -GY, 1))
+        high_w, high_p = face(beyond - c)
+        yl_w, yl_p = face(c - jnp.where(y_first, 0.0, roll(c, 1, 1)))
+        yh_w, yh_p = face(jnp.where(y_last, 0.0, roll(c, -1, 1)) - c)
+        zl_w, zl_p = face(c - f_it[t, HALO - 1 : HALO - 1 + W])
+        zh_w, zh_p = face(f_it[t, HALO + 1 : HALO + 1 + W] - c)
+        rea = f_rea[t]
+        diagonal = rea + low_w + high_w + yl_w + yh_w + zl_w + zh_w
+        w0[F_DG, t] = diagonal
+        w0[F_INV, t] = 1.0 / diagonal
+        w0[F_XM, t] = jnp.where(x_first, 0.0, low_w) if t == 0 else low_w
+        w0[F_XP, t] = jnp.where(x_last, 0.0, high_w) if t == X - 1 else high_w
+        w0[F_YM, t] = jnp.where(y_first, 0.0, yl_w)
+        w0[F_YP, t] = jnp.where(y_last, 0.0, yh_w)
+        w0[F_ZM, t] = jnp.where(z_low, zl_w, 0.0)
+        w0[F_ZP, t] = jnp.where(z_high, zh_w, 0.0)
+        r = f_src[t] - rea * c + (high_p - low_p) + (yh_p - yl_p) + (zh_p - zl_p)
+        r = jnp.where(inside, r, 0.0)
+        az[t] = r
+        r_ref[t] = r
+        low_w, low_p = high_w, high_p
+
+    def coarsen(get, step):
+        def build(k):
+            def both(field, t):
+                low, high = get(field, t)
+                return low + high
+            lo, hi = 2 * k, 2 * k + 1
+            xm = pair(both(F_XM, lo), step)
+            ym_all = both(F_YM, lo) + both(F_YM, hi)
+            zl0, zh0 = get(F_ZM, lo)
+            zl1, zh1 = get(F_ZM, hi)
+            between = pair(both(F_XM, hi), step) + pick_high(ym_all, step) + pair(zh0 + zh1, step)
+            diagonal = pair(both(F_DG, lo) + both(F_DG, hi), step) - 2.0 * between
+            return diagonal, xm, pick_low(ym_all, step), pair(zl0 + zl1, step)
+        return build
+
+    n1 = W // 2
+    S1 = S // 2
+    W1 = S1 + 2 * HALO
+    T1 = X // 2
+    at1 = (W1 - n1) // 2
+
+    def halves0(field, t):
+        return w0[field, t, pl.ds(0, n1, stride=2)], w0[field, t, pl.ds(1, n1, stride=2)]
+
+    for k in range(T1):
+        for field, value in zip((F_DG, F_XM, F_YM, F_ZM), coarsen(halves0, 1)(k)):
+            w1[field, k, at1 : at1 + n1] = value
+
+    def complete1():
+        for k in range(T1):
+            w1[F_INV, k] = 1.0 / w1[F_DG, k]
+            w1[F_XP, k] = w1[F_XM, k + 1] if k < T1 - 1 else roll(w1[F_XM, 0], -GY, 1)
+            w1[F_YP, k] = roll(w1[F_YM, k], -2, 1)
+            w1[F_ZP, k] = roll(w1[F_ZM, k], -1, 0)
+
+    complete1()
+
+    S2 = S // 4
+    T2 = X // 4
+
+    def halves1(field, t):
+        return w1[field, t, pl.ds(HALO, S2, stride=2)], w1[field, t, pl.ds(HALO + 1, S2, stride=2)]
+
+    own_chunk = lax.rem(lane(S2), S2) == row(S2)
+
+    def pack(v):
+        return jnp.sum(jnp.where(own_chunk, v, 0.0), axis=0, keepdims=True)
+
+    for k in range(T2):
+        for field, value in zip((F_DG, F_XM, F_YM, F_ZM), coarsen(halves1, 2)(k)):
+            wmsg[field * T2 + k : field * T2 + k + 1] = pack(value)
+
+    def laps(w, vs, t, step):
+        T, n = w.shape[1], w.shape[2]
+        mid = slice(HALO, HALO + n)
+        weights = [w[field, t] for field in range(F_INV)]
+        out = []
+        for v in vs:
+            c = v[t, mid]
+            below = v[t - 1, mid] if t > 0 else roll(v[T - 1, mid], GY, 1)
+            above = v[t + 1, mid] if t < T - 1 else roll(v[0, mid], -GY, 1)
+            acc = weights[F_DG] * c - weights[F_XM] * below - weights[F_XP] * above
+            acc = acc - weights[F_YM] * roll(c, step, 1) - weights[F_YP] * roll(c, -step, 1)
+            acc = acc - weights[F_ZM] * v[t, HALO - 1 : HALO - 1 + n]
+            out.append(acc - weights[F_ZP] * v[t, HALO + 1 : HALO + 1 + n])
+        return out
+
+    def lap(w, v, t, step):
+        return laps(w, [v], t, step)[0]
+
+    def centre(v, t, n):
+        return v[t, HALO : HALO + n]
+
+    def before(w, fields, step):
+        T, n = w.shape[1], w.shape[2]
+        mid = slice(HALO, HALO + n)
+        for t in range(T):
+            inverse = w[F_INV, t]
+            for r_of, u1, _, _, _, _ in fields:
+                u1[t, mid] = inverse * r_of[t] * (1.0 / MID)
+        for t in range(T):
+            images = laps(w, [f[1] for f in fields], t, step)
+            inverse = w[F_INV, t]
+            for image, (r_of, u1, u2, rem1, s_out, _) in zip(images, fields):
+                r = r_of[t] - image
+                first = centre(u1, t, n)
+                u = C_ONE * first + C_TWO * inverse * r
+                u2[t, mid] = u
+                s_out[t] = first + u
+                rem1[t] = r
+        for t in range(T):
+            images = laps(w, [f[2] for f in fields], t, step)
+            for image, (_, _, _, rem1, _, r_out) in zip(images, fields):
+                r_out[t] = rem1[t] - image
+
+    def after(w, e, u1, rem1, s_in, r_in, put, step):
+        T, n = w.shape[1], w.shape[2]
+        mid = slice(HALO, HALO + n)
+        for t in range(T):
+            r = r_in[t] - lap(w, e, t, step)
+            rem1[t] = r
+            u1[t, mid] = w[F_INV, t] * r * (1.0 / MID)
+        for t in range(T):
+            r = rem1[t] - lap(w, u1, t, step)
+            u = centre(u1, t, n)
+            put(t, s_in[t] + centre(e, t, n) + u + (C_ONE * u + C_TWO * w[F_INV, t] * r))
+
+    fine = ((az, va, vb, rr, sa, ra), (r_ref, vc, vd, rs, sb, rb))
+    coarse = ((r1in, ua, ub, rr1, sa1, ra1), (r1by, uc, ud, rs1, sb1, rb1))
+    C_ROW = (0, T2 + 1)
+
+    def presmooth(par, many):
+        before(w0, fine[:many], 1)
+        for f in range(many):
+            rem = fine[f][-1]
+            for k in range(T1):
+                total = None
+                for t in (2 * k, 2 * k + 1):
+                    part = rem[t, pl.ds(0, n1, stride=2)] + rem[t, pl.ds(1, n1, stride=2)]
+                    total = part if total is None else total + part
+                coarse[f][0][k, at1 : at1 + n1] = pair(total, 1)
+        before(w1, coarse[:many], 2)
+        for f in range(many):
+            rem = coarse[f][-1]
+            for k in range(T2):
+                total = None
+                for t in (2 * k, 2 * k + 1):
+                    part = rem[t, pl.ds(HALO, S2, stride=2)] + rem[t, pl.ds(HALO + 1, S2, stride=2)]
+                    total = part if total is None else total + part
+                msg[par, C_ROW[f] + k : C_ROW[f] + k + 1] = pack(pair(total, 2))
+
+    def all_others(make):
+        for other in range(nx * ny * nz):
+            @pl.when(me != other)
+            def _():
+                make((other // (ny * nz), other // nz % ny, other % nz)).start()
+
+    def spread_message(par):
+        gath[par, slab] = msg[par]
+        all_others(lambda dev: pltpu.make_async_remote_copy(
+            src_ref=msg.at[par], dst_ref=gath.at[par, slab],
+            send_sem=g_ssem.at[par], recv_sem=g_rsem.at[par],
+            device_id=dev, device_id_type=MESH,
+        ))
+
+    def wait_message(par):
+        others = gath.at[par, pl.ds(0, NS - 1)]
+        pltpu.make_async_copy(others, others, g_rsem.at[par]).wait()
+        pltpu.make_async_copy(others, others, g_ssem.at[par]).wait()
+        for s in range(NS):
+            rows_of[s * HALO : s * HALO + 2 * T2 + 1] = gath[par, s]
+
+    def gathered(k):
+        return rows_of[pl.ds(k, NS, stride=HALO)]
+
+    per = 2 * (X + T1)
+    halo_parts = tuple(
+        part for f in range(2) for part in (
+            (coarse[f][4], f * per, T1, S1), (coarse[f][5], f * per + T1, T1, S1),
+            (fine[f][4], f * per + 2 * T1, X, S), (fine[f][5], f * per + 2 * T1 + X, X, S),
+        )
+    )
+
+    def halo_send(par, many):
+        for side, there, dev in ((0, has_lo, lo_dev), (1, has_hi, hi_dev)):
+            @pl.when(there)
+            def _():
+                for ref, first, count, size in halo_parts[: 4 * many]:
+                    start_row = HALO if side == 0 else size
+                    pltpu.make_async_remote_copy(
+                        src_ref=ref.at[:, pl.ds(start_row, HALO)],
+                        dst_ref=hb.at[par, 1 - side, pl.ds(first, count)],
+                        send_sem=h_ssem.at[par, side],
+                        recv_sem=h_rsem.at[par, 1 - side],
+                        device_id=dev,
+                        device_id_type=MESH,
+                    ).start()
+
+    def halo_wait(par, many):
+        for side, there in ((0, has_lo), (1, has_hi)):
+            @pl.when(there)
+            def _():
+                view = hb.at[par, side, pl.ds(0, per * many)]
+                pltpu.make_async_copy(view, view, h_rsem.at[par, side]).wait()
+                pltpu.make_async_copy(view, view, h_ssem.at[par, side]).wait()
+
+    chunk = lax.rem(lane(NS), S2)
+
+    def down2(v):
+        return jnp.where(chunk == 0, roll(roll(v, 1 - S2, 1), 1, 0), roll(v, 1, 1))
+
+    def up2(v):
+        return jnp.where(chunk == S2 - 1, roll(roll(v, S2 - 1, 1), -1, 0), roll(v, -1, 1))
+
+    def down3(v):
+        return jnp.where(chunk < S2 // 2, roll(roll(v, -(S2 // 2), 1), 1, 0), roll(v, S2 // 2, 1))
+
+    def up3(v):
+        return jnp.where(chunk >= S2 // 2, roll(roll(v, S2 // 2, 1), -1, 0), roll(v, -(S2 // 2), 1))
+
+    def lap_all(w, vs, step, down, up):
+        T = len(vs)
+        out = []
+        for t in range(T):
+            v = vs[t]
+            below = vs[t - 1] if t > 0 else roll(vs[T - 1], GY, 1)
+            above = vs[t + 1] if t < T - 1 else roll(vs[0], -GY, 1)
+            acc = w[F_DG, t] * v - w[F_XM, t] * below - w[F_XP, t] * above
+            acc = acc - w[F_YM, t] * roll(v, step, 1) - w[F_YP, t] * roll(v, -step, 1)
+            out.append(acc - w[F_ZM, t] * down(v) - w[F_ZP, t] * up(v))
+        return out
+
+    def complete_all(w, step, up):
+        T = w.shape[1]
+        for t in range(T):
+            w[F_INV, t] = 1.0 / w[F_DG, t]
+            w[F_XP, t] = w[F_XM, t + 1] if t < T - 1 else roll(w[F_XM, 0], -GY, 1)
+            w[F_YP, t] = roll(w[F_YM, t], -step, 1)
+            w[F_ZP, t] = up(w[F_ZM, t])
+
+    def world():
+        def apply2(v):
+            return lap_all(w2, v, S2, down2, up2)
+
+        def apply3(v):
+            return lap_all(w3, v, 2 * S2, down3, up3)
+
+        def scaled(w, r):
+            return [w[F_INV, t] * r[t] for t in range(len(r))]
+
+        def minus(a, b):
+            return [x - y for x, y in zip(a, b)]
+
+        def plus(*many):
+            return [sum(vs[1:], vs[0]) for vs in zip(*many)]
+
+        def first(w, r):
+            return [d * (1.0 / MID) for d in scaled(w, r)]
+
+        def follow(w, u, r, one, two):
+            return [one * a + two * d for a, d in zip(u, scaled(w, r))]
+
+        r = [cres[k] for k in range(T2)]
+        u = first(w2, r)
+        r = minus(r, apply2(u))
+        u2 = follow(w2, u, r, C_ONE, C_TWO)
+        total = plus(u, u2)
+        r = minus(r, apply2(u2))
+        rc = [pair(pair(r[0] + r[1], S2), 1)]
+        u = first(w3, rc)
+        rc = minus(rc, apply3(u))
+        v = follow(w3, u, rc, C_ONE, C_TWO)
+        e = plus(u, v)
+        rc = minus(rc, apply3(v))
+        e = plus(e, follow(w3, v, rc, C_THREE, C_FOUR))
+        e = [e[0]] * T2
+        total = plus(total, e)
+        r = minus(r, apply2(e))
+        u = first(w2, r)
+        r = minus(r, apply2(u))
+        total = plus(total, u, follow(w2, u, r, C_ONE, C_TWO))
+        for k in range(T2):
+            e2[k, HALO : HALO + NS] = total[k]
+
+    def precondition():
+        world()
+        for d in range(3):
+            for k in range(T2):
+                line = e2[k, pl.ds(slab + HALO - 1 + d, 1)]
+                v = jnp.where(own_chunk, jnp.broadcast_to(line, (S2, LANES)), 0.0)
+                v = pair(pair(v, 1), 2)
+                for t in (2 * k, 2 * k + 1):
+                    for half in range(2):
+                        ua[t, pl.ds(HALO + 2 * S2 * d + half, S2, stride=2)] = v
+
+        def put1(k, v):
+            for t in (2 * k, 2 * k + 1):
+                for half in range(2):
+                    va[t, pl.ds(half, W1, stride=2)] = v
+
+        after(w1, ua, ub, rr1, s1, r1, put1, 2)
+
+        def put0(t, v):
+            vz[t, HALO : HALO + W] = v
+
+        after(w0, va, vb, rr, s0, r0, put0, 1)
+
+    def total_of(v):
+        return jnp.sum(jnp.sum(v, axis=0, keepdims=True), axis=1, keepdims=True)
+
+    lane_1 = lane(1)
+
+    def image_and_dots(par):
+        rz = zaz = zq = None
+        own = slice(HALO, HALO + S)
+        for t in range(X):
+            image = lap(w0, vz, t, 1)
+            az[t] = image
+            z = vz[t, 2 * HALO : 2 * HALO + S]
+            parts = (r_ref[t, own] * z, z * image[own], z * q_ref[t, own])
+            if t == 0:
+                rz, zaz, zq = parts
+            else:
+                rz, zaz, zq = rz + parts[0], zaz + parts[1], zq + parts[2]
+        msg[par, T2 : T2 + 1] = jnp.where(
+            lane_1 == 0, total_of(rz), jnp.where(lane_1 == 1, total_of(zaz), total_of(zq))
+        )
+
+    def lane_of(v, i):
+        return jnp.sum(jnp.where(lane_1 == i, v, 0.0), axis=1, keepdims=True)
+
+    def scalars(rz_old, pq_old):
+        sums = jnp.sum(gathered(T2), axis=0, keepdims=True)
+        rz, zaz, zq = lane_of(sums, 0), lane_of(sums, 1), lane_of(sums, 2)
+        beta = rz / rz_old
+        pq = zaz + 2.0 * beta * zq + beta * beta * pq_old
+        return rz, pq, rz / pq, beta
+
+    def advance(a, beta):
+        for t in range(X):
+            p = vz[t, HALO : HALO + HALO + S] + beta * p_ref[t]
+            p_ref[t] = p
+            dir_ref[t] = dir_ref[t] + a * p
+            q = az[t] + beta * q_ref[t]
+            q_ref[t] = q
+            r_ref[t] = r_ref[t] - a * q
+
+    def coarse_advance(a, beta):
+        for k in range(T2):
+            v = gathered(C_ROW[0] + k) + beta * cq[k]
+            cq[k] = v
+            cres[k] = gathered(C_ROW[1] + k) - a * v
+
+    def kept_advance(par, a, beta):
+        for i, (keep, slope) in enumerate(((s1, sq1), (r1, rq1), (s0, sq), (r0, rq))):
+            moved, first, count, size = halo_parts[i]
+            base, other, _, _ = halo_parts[4 + i]
+            for t in range(count):
+                for rows, got in (
+                    (slice(0, HALO), lambda ref, at: hb[par, 0, at + t]),
+                    (slice(HALO, HALO + size), lambda ref, at: ref[t, HALO : HALO + size]),
+                    (slice(HALO + size, 2 * HALO + size), lambda ref, at: hb[par, 1, at + t]),
+                ):
+                    if a is None:
+                        keep[t, rows] = got(moved, first)
+                    else:
+                        v = got(moved, first) + beta * slope[t, rows]
+                        slope[t, rows] = v
+                        keep[t, rows] = got(base, other) - a * v
+
+    all_others(lambda dev: pltpu.make_async_remote_copy(
+        src_ref=wmsg, dst_ref=wgath.at[pl.ds(pl.multiple_of(slab * HALO, HALO), HALO)],
+        send_sem=g_ssem.at[2], recv_sem=g_rsem.at[2], device_id=dev, device_id_type=MESH,
+    ))
+    wgath[pl.ds(pl.multiple_of(slab * HALO, HALO), HALO)] = wmsg[...]
+    for side, there, dev in ((0, has_lo, lo_dev), (1, has_hi, hi_dev)):
+        @pl.when(there)
+        def _():
+            pltpu.make_async_remote_copy(
+                src_ref=w1.at[pl.ds(0, 4), :, pl.ds(HALO, HALO)], dst_ref=sh.at[1 - side],
+                send_sem=h_ssem.at[2, side], recv_sem=h_rsem.at[2, 1 - side],
+                device_id=dev, device_id_type=MESH,
+            ).start()
+    presmooth(0, 1)
+    msg[0, T2:] = jnp.zeros((T2 + 1, LANES), f32)
+    spread_message(0)
+    halo_send(0, 1)
+
+    for a in range(len(arrays)):
+        for wanted, copy in pieces(a):
+            @pl.when(wanted)
+            def _():
+                copy.wait_send()
+
+    others = wgath.at[pl.ds(0, (NS - 1) * HALO)]
+    pltpu.make_async_copy(others, others, g_rsem.at[2]).wait()
+    pltpu.make_async_copy(others, others, g_ssem.at[2]).wait()
+    for field in range(4):
+        for k in range(T2):
+            w2[field, k] = wgath[pl.ds(field * T2 + k, NS, stride=HALO)]
+    complete_all(w2, S2, up2)
+    dg, xm, ym, zm = F_DG, F_XM, F_YM, F_ZM
+    ym_all = w2[ym, 0] + w2[ym, 1]
+    ym_all = pair(ym_all, 1)
+    zm_all = pair(w2[zm, 0] + w2[zm, 1], S2)
+    between = pair(pair(w2[xm, 1], S2), 1) + pick_high(ym_all, S2) + pick_high(zm_all, 1)
+    w3[dg, 0] = pair(pair(w2[dg, 0] + w2[dg, 1], S2), 1) - 2.0 * between
+    w3[xm, 0] = pair(pair(w2[xm, 0], S2), 1)
+    w3[ym, 0] = pick_low(ym_all, S2)
+    w3[zm, 0] = pick_low(zm_all, 1)
+    complete_all(w3, 2 * S2, up3)
+    for side, there in ((0, has_lo), (1, has_hi)):
+        @pl.when(there)
+        def _():
+            view = sh.at[side]
+            pltpu.make_async_copy(view, view, h_rsem.at[2, side]).wait()
+            pltpu.make_async_copy(view, view, h_ssem.at[2, side]).wait()
+            first = 0 if side == 0 else HALO + S1
+            for field in range(4):
+                w1[field, :, first : first + HALO] = sh[side, field]
+    complete1()
+    wait_message(0)
+    for k in range(T2):
+        cres[k] = gathered(k)
+    halo_wait(0, 1)
+    kept_advance(0, None, None)
+
+    def body(it_idx, carry):
+        par = lax.rem(it_idx + 1, 2)
+        precondition()
+        image_and_dots(par)
+        presmooth(par, 2)
+        spread_message(par)
+        halo_send(par, 2)
+        wait_message(par)
+        rz, pq, a, beta = scalars(*carry)
+        coarse_advance(a, beta)
+        advance(a, beta)
+        halo_wait(par, 2)
+        kept_advance(par, a, beta)
+        return rz, pq
+
+    one = jnp.ones((1, 1), f32)
+    carry = lax.fori_loop(0, ITERS - 1, body, (one, jnp.zeros((1, 1), f32)))
+    last = ITERS % 2
+    precondition()
+    image_and_dots(last)
+    spread_message(last)
+    wait_message(last)
+    _, _, a, beta = scalars(*carry)
+    advance(a, beta)
+
+    def back_copy(which, jd):
+        dev = device_at(jd, iz)
+        return pltpu.make_async_remote_copy(
+            src_ref=outs.at[which, dev[0] * ny + dev[1]],
+            dst_ref=back.at[which, pl.ds(pl.multiple_of(S * j, HALO), S)],
+            send_sem=d_ssem.at[which, MID_PART, jd],
+            recv_sem=d_rsem.at[which, MID_PART],
+            device_id=dev,
+            device_id_type=MESH,
+        )
+
+    for which in range(2):
+        for at in range(0, S, HALO):
+            if which == 0:
+                tiles = [dir_ref[t, HALO + at : 2 * HALO + at] for t in range(X)]
+            else:
+                tiles = [r_ref[t, HALO + at : 2 * HALO + at] for t in range(X)]
+            tiles = block_transpose(tiles)
+            for t in range(X):
+                outs[which, t, at : at + HALO] = tiles[t]
+        for jd in range(P):
+            @pl.when(j != jd)
+            def _():
+                back_copy(which, jd).start()
+        back[which, pl.ds(pl.multiple_of(S * j, HALO), S)] = outs[which, own_tile]
+
+    def energy(g):
+        square = 1.0 + g * g
+        return (square * jnp.sqrt(square) - 1.0) * (1.0 / 3.0)
+
+    lanes = lane(S)
+    y_at = lax.rem(lanes, GY)
+    x_first, x_last, y_first = lanes < GY, lanes >= LANES - GY, y_at == 0
+    ends = jnp.where(y_at == GY - 1, 1.0, 0.0) + jnp.where(slab * S + row(S) == NZ - 1, 1.0, 0.0)
+    ends_x = ends + jnp.where(x_last, 1.0, 0.0)
+    fetch = lax.rem(lane_1, GY)
+    packed = jnp.zeros((1, LANES), f32)
+    for k in range(TRIALS):
+        s = jnp.exp2(-jnp.full((1, LANES), tp_ref[k], jnp.int32).astype(f32))
+
+        def trial(t, shift):
+            first = 2 * HALO - shift
+            return f_it[t, first : first + S] + s * dir_ref[t, HALO - shift : HALO - shift + S]
+
+        below = jnp.where(x_first, 0.0, roll(trial(X - 1, 0), GY, 1))
+        for t in range(X):
+            v = trial(t, 0)
+            e = energy(v - below) + energy(v - trial(t, 1))
+            e = e + energy(v - jnp.where(y_first, 0.0, roll(v, 1, 1)))
+            e = e + energy(v) * (ends_x if t == X - 1 else ends)
+            e = e + (0.5 * f_rea[t, HALO : HALO + S] * v - f_src[t, HALO : HALO + S]) * v
+            column = jnp.sum(e, axis=0, keepdims=True)
+            step = 1
+            while step < GY:
+                column = pair(column, step)
+                step *= 2
+            packed = packed + jnp.where(fetch == k * X + t, column, 0.0)
+            below = v
+    emsg[...] = packed
+    egath[slab] = packed
+    all_others(lambda dev: pltpu.make_async_remote_copy(
+        src_ref=emsg, dst_ref=egath.at[slab],
+        send_sem=g_ssem.at[3], recv_sem=g_rsem.at[3], device_id=dev, device_id_type=MESH,
+    ))
+    for which, out in ((0, dir_out), (1, rem_out)):
+        view = back.at[which, pl.ds(0, S * (P - 1))]
+        pltpu.make_async_copy(view, view, d_rsem.at[which, MID_PART]).wait()
+        out[...] = back[which].T.reshape(X, Y, Z)
+        for jd in range(P):
+            @pl.when(j != jd)
+            def _():
+                back_copy(which, jd).wait_send()
+    others = egath.at[pl.ds(0, NS - 1)]
+    pltpu.make_async_copy(others, others, g_rsem.at[3]).wait()
+    pltpu.make_async_copy(others, others, g_ssem.at[3]).wait()
+    layers = jnp.sum(egath[...], axis=0) / (GY * NZ)
+    here = jnp.where(lane_1 // GY == ix, layers, 0.0)
+    at_k = lax.broadcasted_iota(jnp.int32, (TRIALS * X, LANES), 0)
+    mine = jnp.sum(jnp.where(lax.rem(lane(TRIALS * X), GY) == at_k, here, 0.0), axis=1, keepdims=True)
+    mine = jnp.where(lane(TRIALS * X) == lax.rem(at_k, X), mine, 0.0)
+    for k in range(TRIALS):
+        le_ref[k : k + 1] = jnp.sum(mine[k * X : k * X + X], axis=0, keepdims=True)[:, :X]
+        total = jnp.sum(jnp.where(fetch // X == k, layers, 0.0), axis=1, keepdims=True) / (X * nx)
+        en_ref[k : k + 1] = jnp.broadcast_to(total, (1, LANES))
+
+
+def slab_on_device(counts, iterate, source, reaction, trial_powers):
+    X, Y, Z = iterate.shape
+    nx, ny, nz = counts
+    P = nx * ny
+    S = Z // P
+    NS = nz * P
+    W, W1 = S + 2 * HALO, S // 2 + 2 * HALO
+    T1, T2, T3 = X // 2, X // 4, X // 8
+    f32 = jnp.float32
+
+    def vm(*shape):
+        return pltpu.VMEM(shape, f32)
+
+    def sem(*shape):
+        return pltpu.SemaphoreType.DMA(shape)
+
+    full, padded = (X, W, LANES), (X, W + 2 * HALO, LANES)
+    full1, padded1 = (T1, W1, LANES), (T1, W1 + 2 * HALO, LANES)
+    scratch = [vm(3, Z, LANES), vm(P, S + 4 * HALO, LANES), vm(P, W, LANES), vm(P, W, LANES)]
+    scratch += [vm(*padded), vm(*full), vm(*full)]
+    scratch += [vm(8, *full), vm(8, *full1), vm(8, T2, NS, LANES), vm(8, T3, NS, LANES)]
+    scratch += [vm(*padded)] * 5 + [vm(*full)] * 11
+    scratch += [vm(*padded1)] * 4 + [vm(*full1)] * 12
+    scratch += [vm(T2, NS + 2 * HALO, LANES), vm(T2, NS, LANES), vm(T2, NS, LANES)]
+    scratch += [vm(X, S + HALO, LANES)] * 2 + [vm(*full)] * 2
+    scratch += [vm(2, 2 * T2 + 1, LANES), vm(2, NS, 2 * T2 + 1, LANES), vm(NS * HALO, LANES)]
+    scratch += [vm(HALO, LANES), vm(NS * HALO, LANES)]
+    scratch += [vm(2, 2, 4 * (X + T1), HALO, LANES), vm(2, 4, T1, HALO, LANES)]
+    scratch += [vm(1, LANES), vm(NS, 1, LANES), vm(2, P, S, LANES), vm(2, Z, LANES)]
+    scratch += [sem(3, 3, P), sem(3, 3), sem(4), sem(4), sem(3, 2), sem(3, 2)]
+    whole = pl.BlockSpec(memory_space=pltpu.VMEM)
+    out = pl.pallas_call(
+        functools.partial(slab_kernel, (X, Y, Z), counts),
+        out_shape=[
+            jax.ShapeDtypeStruct((X, Y, Z), f32),
+            jax.ShapeDtypeStruct((X, Y, Z), f32),
+            jax.ShapeDtypeStruct((TRIALS, X), f32),
+            jax.ShapeDtypeStruct((TRIALS, LANES), f32),
+        ],
+        in_specs=[pl.BlockSpec(memory_space=pltpu.SMEM), whole, whole, whole],
+        out_specs=[whole] * 4,
+        scratch_shapes=scratch,
+        compiler_params=pltpu.CompilerParams(has_side_effects=True, vmem_limit_bytes=48 * 1024 * 1024),
+        name="newton_step",
+    )(trial_powers, iterate, source, reaction)
+    return out[0], out[1], out[2], out[3][:, 0]
+
+
 def solution(mesh):
     counts = tuple(mesh.shape[axis] for axis in ("gx", "gy", "gz"))
     grid = P("gx", "gy", "gz")
+
+    def on_each(iterate, source, reaction, trial_powers):
+        form = slab_on_device if slab_fits(counts, iterate.shape) else on_device
+        return form(counts, iterate, source, reaction, trial_powers)
+
     return jax.shard_map(
-        functools.partial(on_device, counts),
+        on_each,
         mesh=mesh,
         in_specs=(grid, grid, grid, P()),
         out_specs=(grid, grid, P(None, "gx"), P()),

time: 176 us -> 80.8 us (0.46)
  Pallas kernels: 170 us -> 74.2 us
    pallas_call x1, Pallas kernels: 170 us -> 74.2 us  [slab_on_device(): pl.pallas_call(functools.partial(slab_kernel, (X, Y, Z), counts), out_sha...]
where the time goes in v1:
time: 80.8 us; the launch traced here: 80.5 us
  Pallas kernels  74.2 us (92%)
  local copies, waits for them, and re-layouts  5.63 us (7%)
    pallas_call x1, Pallas kernels, slab_on_device(): pl.pallas_call(functools.partial(slab_kernel, (X, Y, Z), counts), out_sha...  74.2 us
    unnamed x11, local copies, waits for them, and re-layouts  5 us

profile of v1, /device:TPU:0, one launch (start us, length us, event | category | flops | bytes accessed | tf_op | source)
XLA Modules:
  0.0 80.5 jit_solution(2087683452532404874)
XLA Ops:
  0.6 0.0 copy-start
  0.6 0.8 %copy-done = f32[8,16,128]{2,1,0:T(8,128)S(1)} copy-done((f32[8,16,128]{2,1,0:T(8,128)S(1)}, f32[8,16,128]{2,1,0:T(8,128)}, u32[]{:S(2)}) %copy-start) | copy-done | bytes 65560
  1.5 0.0 copy-start.1
  1.5 0.8 %copy-done.1 = f32[8,16,128]{2,1,0:T(8,128)S(1)} copy-done((f32[8,16,128]{2,1,0:T(8,128)S(1)}, f32[8,16,128]{2,1,0:T(8,128)}, u32[]{:S(2)}) %copy-start.1) | copy-done | bytes 65560
  2.3 0.0 copy-start.2
  2.3 0.8 %copy-done.2 = f32[8,16,128]{2,1,0:T(8,128)S(1)} copy-done((f32[8,16,128]{2,1,0:T(8,128)S(1)}, f32[8,16,128]{2,1,0:T(8,128)}, u32[]{:S(2)}) %copy-start.2) | copy-done | bytes 65560
  3.2 0.0 copy-start.3
  3.2 0.7 copy-done.3
  3.8 74.2 %newton_step.1 = (f32[8,16,128]{2,1,0:T(8,128)S(1)}, f32[8,16,128]{2,1,0:T(8,128)S(1)}, f32[4,8]{1,0:T(4,128)S(1)}, f32[4,128]{1,0:T(4,128)S(1)}) custom-call(s32[4]{0:T(128)S(1)} %copy-done.3, f32[8,16,128]{2,1,0:T(8,128)S(1)} %copy-done, f32[8,16,128]{2,1,0:T(8,128)S(1)} %copy-done.1, f32[8,16,128]{2,1,0:T(8,128)S(1)} %copy-done.2), custom_call_target="tpu_custom_call" | custom-call | tf_op jit(solution)/shard_map/newton_step/pallas_call | solution.py:1296
  78.1 0.6 slice_reduce_fusion
  78.7 0.6 copy.11
  79.3 0.6 copy.12
  79.9 0.6 copy.13
Async XLA Ops:
  0.6 0.8 %copy-start = (f32[8,16,128]{2,1,0:T(8,128)S(1)}, f32[8,16,128]{2,1,0:T(8,128)}, u32[]{:S(2)}) copy-start(f32[8,16,128]{2,1,0:T(8,128)} %it_in.1) | copy-start | bytes 196612
  1.5 0.8 %copy-start.1 = (f32[8,16,128]{2,1,0:T(8,128)S(1)}, f32[8,16,128]{2,1,0:T(8,128)}, u32[]{:S(2)}) copy-start(f32[8,16,128]{2,1,0:T(8,128)} %src_in.1) | copy-start | bytes 196612
  2.3 0.8 %copy-start.2 = (f32[8,16,128]{2,1,0:T(8,128)S(1)}, f32[8,16,128]{2,1,0:T(8,128)}, u32[]{:S(2)}) copy-start(f32[8,16,128]{2,1,0:T(8,128)} %rea_in.1) | copy-start | bytes 196612
  3.2 0.7 copy-start.3

commit v2 on v0

--- a/solution.py
+++ b/solution.py
@@ -535,11 +535,849 @@
     return out[0], out[1], out[2], out[3][:, 0]
 
 
+LANES = 128
+HALO = 8
+PLANES = 2
+PAIR = 2
+CHUNK = 4
+F_DG, F_XM, F_YM, F_ZM, F_XP, F_YP, F_ZP, F_INV = range(8)
+C_ONE = RHO1 * RHO0
+C_TWO = 2.0 * RHO1 / HALF
+C_THREE = RHO2 * RHO1
+C_FOUR = 2.0 * RHO2 / HALF
+
+
+def slab_fits(counts, shape):
+    X, Y, Z = shape
+    nx, ny, nz = counts
+    per = PLANES * ny * PAIR
+    rows = PAIR * Z // per
+    return (
+        X == 1 << (LEVELS - 1) and X * Y == LANES and nx * ny == X and nx >= PLANES and nz % PAIR == 0
+        and rows * per == PAIR * Z and rows % (2 * HALO) == 0 and Z % rows == 0
+    )
+
+
+def slab_kernel(
+    sizes, counts, tp_ref, it_in, src_in, rea_in, dir_out, rem_out, le_ref, en_ref,
+    turned, d_it, d_rs, f_it, f_rea, f_src, w0, w1, w2, w3,
+    va, vb, vz, rr, az, sa, ra, sb, rb, s0, r0, sq, rq,
+    ua, ub, r1in, rr1, sa1, ra1, sb1, rb1, s1, r1, sq1, rq1, e2, cres, cq, cnew,
+    p_ref, dir_ref, q_ref, r_ref,
+    msg, gath, early, egath, wmsg, wgath, hb, he, sh, enmsg, engath, outs, back,
+    d_ssem, d_rsem, g_ssem, g_rsem, h_ssem, h_rsem, b_ssem, b_rsem, e_ssem,
+):
+    X, Y, Z = sizes
+    nx, ny, nz = counts
+    P = nx * ny
+    GY = ny * Y
+    NZ = nz * Z
+    PER = PLANES * ny
+    NS = PER * nz
+    S = NZ // NS
+    BLOCK = Z // S
+    W = S + 2 * HALO
+    f32 = jnp.float32
+    ix, iy, iz = lax.axis_index("gx"), lax.axis_index("gy"), lax.axis_index("gz")
+    me = (ix * ny + iy) * nz + iz
+    own_tile = ix * ny + iy
+    base = (nx - PLANES) // 2
+
+    def fold(value, turn, size):
+        return value + lax.rem(turn, 2) * (size - 1 - 2 * value)
+
+    def device_of(s):
+        c = s // PAIR
+        plane = c // PER
+        q = fold(lax.rem(c, PER), plane, PER)
+        y = q // PLANES
+        return (base + fold(lax.rem(q, PLANES), y, PLANES), y, plane * PAIR + lax.rem(s, PAIR))
+
+    works = jnp.logical_and(ix >= base, ix < base + PLANES)
+    plane = iz // PAIR
+    slab = fold(iy * PLANES + fold(ix - base, iy, PLANES), plane, PER)
+    slab = (plane * PER + slab) * PAIR + lax.rem(iz, PAIR)
+    slab = jnp.where(works, slab, -BLOCK - 1)
+    block = slab // BLOCK
+    j = lax.rem(slab, BLOCK)
+
+    has_lo, has_hi = slab > 0, slab < NS - 1
+    lo_dev, hi_dev = device_of(jnp.maximum(slab - 1, 0)), device_of(jnp.clip(slab + 1, 0, NS - 1))
+
+    def lane(n):
+        return lax.broadcasted_iota(jnp.int32, (n, LANES), 1)
+
+    def row(n):
+        return lax.broadcasted_iota(jnp.int32, (n, LANES), 0)
+
+    def low_bit(n, step):
+        return lax.rem(lane(n), 2 * step) < step
+
+    def swap(v, step):
+        return jnp.where(low_bit(v.shape[0], step), roll(v, -step, 1), roll(v, step, 1))
+
+    def pair(v, step):
+        return v + swap(v, step)
+
+    def pick_low(v, step):
+        return jnp.where(low_bit(v.shape[0], step), v, roll(v, step, 1))
+
+    def pick_high(v, step):
+        return jnp.where(low_bit(v.shape[0], step), roll(v, -step, 1), v)
+
+    def block_transpose(tiles):
+        n = tiles[0].shape[0]
+        k = P // 2
+        while k:
+            low = low_bit(n, Y * k)
+            new = list(tiles)
+            for i in range(P):
+                if not i & k:
+                    a, b = tiles[i], tiles[i | k]
+                    new[i] = jnp.where(low, a, roll(b, Y * k, 1))
+                    new[i | k] = jnp.where(low, roll(a, -Y * k, 1), b)
+            tiles = new
+            k //= 2
+        return tiles
+
+    parts = ((pl.ds(0, 1), d_it, 2 * HALO), (pl.ds(1, 2), d_rs, HALO))
+
+    def pieces(a):
+        halo = parts[a][2]
+        for jd in range(BLOCK):
+            first = S * jd - (halo if jd > 0 else 0)
+            last = S * jd + S + (halo if jd < BLOCK - 1 else 0)
+            yield BLOCK * iz + jd, None, first, last - first, 0 if jd > 0 else halo, jd
+        yield BLOCK * iz + BLOCK, iz < nz - 1, Z - halo, halo, 0, BLOCK
+        yield BLOCK * iz - 1, iz > 0, 0, halo, halo + S, BLOCK + 1
+
+    def piece(a, to, first, count, there, number):
+        which, landed, _ = parts[a]
+        return pltpu.make_async_remote_copy(
+            src_ref=turned.at[which, pl.ds(first, count)],
+            dst_ref=landed.at[:, own_tile, pl.ds(there, count)],
+            send_sem=d_ssem.at[a, number],
+            recv_sem=d_rsem.at[a, max(number - BLOCK + 1, 0)],
+            device_id=device_of(jnp.clip(to, 0, NS - 1)),
+            device_id_type=MESH,
+        )
+
+    def both(a, b):
+        return b if a is None else jnp.logical_and(a, b)
+
+    @pl.when(works)
+    def _():
+        for ref in (va, vb, vz, ua, ub, r1in, e2, p_ref, dir_ref, q_ref, sq, rq, sq1, rq1, cq, w1):
+            ref[...] = jnp.zeros_like(ref)
+        w1[F_DG] = jnp.ones(w1.shape[1:], f32)
+        for side, at in ((0, 0), (1, NS - 1)):
+            @pl.when(slab == at)
+            def _():
+                for ref in (hb, he):
+                    ref[:, side] = jnp.zeros(ref.shape[:1] + ref.shape[2:], f32)
+
+    for a, (which, landed, halo) in enumerate(parts):
+        for i, given in ((0, it_in),) if a == 0 else ((1, rea_in), (2, src_in)):
+            turned[i] = given[...].reshape(LANES, Z).T
+        for to, exists, first, count, there, number in pieces(a):
+            @pl.when(both(exists, to != slab))
+            def _():
+                piece(a, to, first, count, there, number).start()
+
+            @pl.when(both(exists, to == slab))
+            def _():
+                landed[:, own_tile, there : there + count] = turned[which, first : first + count]
+
+    def wait_sent():
+        for a in range(2):
+            for to, exists, first, count, there, number in pieces(a):
+                @pl.when(both(exists, to != slab))
+                def _():
+                    piece(a, to, first, count, there, number).wait_send()
+
+    def wait_landed(a, wanted, kind, first, count, source):
+        mine = jnp.where(source == iz, 1, 0)
+        for own in range(2):
+            @pl.when(jnp.logical_and(wanted, mine == own))
+            def _():
+                view = parts[a][1].at[:, pl.ds(0, P - own), pl.ds(first, count)]
+                pltpu.make_async_copy(view, view, d_rsem.at[a, kind]).wait()
+
+    def gather_block():
+        for a, (_, landed, halo) in enumerate(parts):
+            @pl.when(slab == 0)
+            def _():
+                landed[:, :, :halo] = jnp.zeros((landed.shape[0], P, halo, LANES), f32)
+
+            @pl.when(slab == NS - 1)
+            def _():
+                landed[:, :, halo + S :] = jnp.zeros((landed.shape[0], P, halo, LANES), f32)
+
+            for jd in range(BLOCK):
+                count = S + (halo if jd > 0 else 0) + (halo if jd < BLOCK - 1 else 0)
+                wait_landed(a, j == jd, 0, 0 if jd > 0 else halo, count, block)
+            wait_landed(a, jnp.logical_and(j == 0, has_lo), 1, 0, halo, block - 1)
+            wait_landed(a, jnp.logical_and(j == BLOCK - 1, has_hi), 2, halo + S, halo, block + 1)
+            for i, flat in ((0, f_it),) if a == 0 else ((0, f_rea), (1, f_src)):
+                for at in range(0, S + 2 * halo, HALO):
+                    tiles = block_transpose([landed[i, t, at : at + HALO] for t in range(P)])
+                    for t in range(P):
+                        flat[t, at : at + HALO] = tiles[t]
+
+    def back_copy(which, t):
+        return pltpu.make_async_remote_copy(
+            src_ref=outs.at[which, t],
+            dst_ref=back.at[which, pl.ds(pl.multiple_of(S * j, HALO), S)],
+            send_sem=b_ssem.at[which, t],
+            recv_sem=b_rsem.at[which],
+            device_id=(t // ny, t % ny, block),
+            device_id_type=MESH,
+        )
+
+    def back_here(which):
+        @pl.when(block == iz)
+        def _():
+            back[which, pl.ds(pl.multiple_of(S * j, HALO), S)] = outs[which, own_tile]
+
+    def energy_copy(dev):
+        return pltpu.make_async_remote_copy(
+            src_ref=enmsg, dst_ref=engath.at[slab],
+            send_sem=e_ssem.at[(dev[0] * ny + dev[1]) * nz + dev[2]], recv_sem=g_rsem.at[5],
+            device_id=dev, device_id_type=MESH,
+        )
+
+    WROWS = 4 * (X // 4) * (S // (4 * CHUNK))
+
+    @pl.when(works)
+    def _():
+        gather_block()
+
+        lanes = lane(W)
+        z_at = slab * S + row(W) - HALO
+        inside = jnp.logical_and(z_at >= 0, z_at < NZ)
+        z_low = jnp.logical_and(z_at > 0, z_at < NZ)
+        z_high = jnp.logical_and(z_at >= 0, z_at < NZ - 1)
+        x_first, x_last = lanes < GY, lanes >= LANES - GY
+        y_at = lax.rem(lanes, GY)
+        y_first, y_last = y_at == 0, y_at == GY - 1
+
+        def face(g):
+            square = g * g
+            root = jnp.sqrt(1.0 + square)
+            return (1.0 + 2.0 * square) / root, g * root
+
+        def window(t):
+            return f_it[t, HALO : HALO + W]
+
+        low_w, low_p = face(window(0) - jnp.where(x_first, 0.0, roll(window(X - 1), GY, 1)))
+        first_w = low_w
+        for t in range(X):
+            c = window(t)
+            beyond = window(t + 1) if t < X - 1 else jnp.where(x_last, 0.0, roll(window(0), -GY, 1))
+            high_w, high_p = face(beyond - c)
+            yl_w, yl_p = face(c - jnp.where(y_first, 0.0, roll(c, 1, 1)))
+            yh_w, yh_p = face(jnp.where(y_last, 0.0, roll(c, -1, 1)) - c)
+            zl_w, zl_p = face(c - f_it[t, HALO - 1 : HALO - 1 + W])
+            zh_w, zh_p = face(f_it[t, HALO + 1 : HALO + 1 + W] - c)
+            rea = f_rea[t]
+            diagonal = rea + low_w + high_w + yl_w + yh_w + zl_w + zh_w
+            w0[F_DG, t] = diagonal
+            w0[F_INV, t] = 1.0 / diagonal
+            w0[F_XM, t] = jnp.where(x_first, 0.0, low_w) if t == 0 else low_w
+            w0[F_XP, t] = jnp.where(x_last, 0.0, high_w) if t == X - 1 else high_w
+            w0[F_YM, t] = jnp.where(y_first, 0.0, yl_w)
+            w0[F_YP, t] = jnp.where(y_last, 0.0, yh_w)
+            w0[F_ZM, t] = jnp.where(z_low, zl_w, 0.0)
+            w0[F_ZP, t] = jnp.where(z_high, zh_w, 0.0)
+            r = f_src[t] - rea * c + (high_p - low_p) + (yh_p - yl_p) + (zh_p - zl_p)
+            r = jnp.where(inside, r, 0.0)
+            az[t] = r
+            r_ref[t] = r
+            low_w, low_p = high_w, high_p
+
+        def coarsen(get, step):
+            def build(k):
+                def both(field, t):
+                    low, high = get(field, t)
+                    return low + high
+                lo, hi = 2 * k, 2 * k + 1
+                xm = pair(both(F_XM, lo), step)
+                ym_all = both(F_YM, lo) + both(F_YM, hi)
+                zl0, zh0 = get(F_ZM, lo)
+                zl1, zh1 = get(F_ZM, hi)
+                between = pair(both(F_XM, hi), step) + pick_high(ym_all, step) + pair(zh0 + zh1, step)
+                diagonal = pair(both(F_DG, lo) + both(F_DG, hi), step) - 2.0 * between
+                return diagonal, xm, pick_low(ym_all, step), pair(zl0 + zl1, step)
+            return build
+
+        n1 = W // 2
+        S1 = S // 2
+        W1 = S1 + 2 * HALO
+        T1 = X // 2
+        at1 = (W1 - n1) // 2
+
+        def halves0(field, t):
+            return w0[field, t, pl.ds(0, n1, stride=2)], w0[field, t, pl.ds(1, n1, stride=2)]
+
+        for k in range(T1):
+            for field, value in zip((F_DG, F_XM, F_YM, F_ZM), coarsen(halves0, 1)(k)):
+                w1[field, k, at1 : at1 + n1] = value
+
+        def complete1():
+            for k in range(T1):
+                w1[F_INV, k] = 1.0 / w1[F_DG, k]
+                w1[F_XP, k] = w1[F_XM, k + 1] if k < T1 - 1 else roll(w1[F_XM, 0], -GY, 1)
+                w1[F_YP, k] = roll(w1[F_YM, k], -2, 1)
+                w1[F_ZP, k] = roll(w1[F_ZM, k], -1, 0)
+
+        complete1()
+
+        S2 = S // 4
+        T2 = X // 4
+        LINES = S2 // CHUNK
+
+        def halves1(field, t):
+            return w1[field, t, pl.ds(HALO, S2, stride=2)], w1[field, t, pl.ds(HALO + 1, S2, stride=2)]
+
+        own_chunk = lax.rem(lane(S2), CHUNK) == lax.rem(row(S2), CHUNK)
+
+        def pack(ref, first, v):
+            v = jnp.where(own_chunk, v, 0.0)
+            for h in range(LINES):
+                ref[first + h : first + h + 1] = jnp.sum(jnp.where(row(S2) // CHUNK == h, v, 0.0), axis=0, keepdims=True)
+
+        for k in range(T2):
+            for field, value in zip((F_DG, F_XM, F_YM, F_ZM), coarsen(halves1, 2)(k)):
+                pack(wmsg, (field * T2 + k) * LINES, value)
+
+        def laps(w, vs, t, step):
+            T, n = w.shape[1], w.shape[2]
+            mid = slice(HALO, HALO + n)
+            weights = [w[field, t] for field in range(F_INV)]
+            out = []
+            for v in vs:
+                c = v[t, mid]
+                below = v[t - 1, mid] if t > 0 else roll(v[T - 1, mid], GY, 1)
+                above = v[t + 1, mid] if t < T - 1 else roll(v[0, mid], -GY, 1)
+                acc = weights[F_DG] * c - weights[F_XM] * below - weights[F_XP] * above
+                acc = acc - weights[F_YM] * roll(c, step, 1) - weights[F_YP] * roll(c, -step, 1)
+                acc = acc - weights[F_ZM] * v[t, HALO - 1 : HALO - 1 + n]
+                out.append(acc - weights[F_ZP] * v[t, HALO + 1 : HALO + 1 + n])
+            return out
+
+        def lap(w, v, t, step):
+            return laps(w, [v], t, step)[0]
+
+        def centre(v, t, n):
+            return v[t, HALO : HALO + n]
+
+        def before(w, r_of, u1, u2, rem1, s_out, r_out, step):
+            T, n = w.shape[1], w.shape[2]
+            mid = slice(HALO, HALO + n)
+            for t in range(T):
+                u1[t, mid] = w[F_INV, t] * r_of[t] * (1.0 / MID)
+            for t in range(T):
+                r = r_of[t] - lap(w, u1, t, step)
+                first = centre(u1, t, n)
+                u = C_ONE * first + C_TWO * w[F_INV, t] * r
+                u2[t, mid] = u
+                s_out[t] = first + u
+                rem1[t] = r
+            for t in range(T):
+                r_out[t] = rem1[t] - lap(w, u2, t, step)
+
+        def after(w, e, u1, rem1, s_in, r_in, put, step):
+            T, n = w.shape[1], w.shape[2]
+            mid = slice(HALO, HALO + n)
+            for t in range(T):
+                r = r_in[t] - lap(w, e, t, step)
+                rem1[t] = r
+                u1[t, mid] = w[F_INV, t] * r * (1.0 / MID)
+            for t in range(T):
+                r = rem1[t] - lap(w, u1, t, step)
+                u = centre(u1, t, n)
+                put(t, s_in[t] + centre(e, t, n) + u + (C_ONE * u + C_TWO * w[F_INV, t] * r))
+
+        kept = ((az, sa, ra, sa1, ra1), (r_ref, sb, rb, sb1, rb1))
+
+        def presmooth(f, ref, par):
+            r_of, s_out, r_out, s1_out, r1_out = kept[f]
+            before(w0, r_of, va, vb, rr, s_out, r_out, 1)
+            for k in range(T1):
+                total = None
+                for t in (2 * k, 2 * k + 1):
+                    part = r_out[t, pl.ds(0, n1, stride=2)] + r_out[t, pl.ds(1, n1, stride=2)]
+                    total = part if total is None else total + part
+                r1in[k, at1 : at1 + n1] = pair(total, 1)
+            before(w1, r1in, ua, ub, rr1, s1_out, r1_out, 2)
+            for k in range(T2):
+                total = None
+                for t in (2 * k, 2 * k + 1):
+                    part = r1_out[t, pl.ds(HALO, S2, stride=2)] + r1_out[t, pl.ds(HALO + 1, S2, stride=2)]
+                    total = part if total is None else total + part
+                pack(ref.at[par], k * LINES, pair(total, 2))
+
+        def to_workers(ref, out, sem):
+            for s in range(NS):
+                @pl.when(slab != s)
+                def _():
+                    pltpu.make_async_remote_copy(
+                        src_ref=ref, dst_ref=out.at[slab], send_sem=g_ssem.at[sem], recv_sem=g_rsem.at[sem],
+                        device_id=device_of(s), device_id_type=MESH,
+                    ).start()
+            out[slab] = ref[...]
+
+        def from_workers(out, sem):
+            others = out.at[pl.ds(0, NS - 1)]
+            pltpu.make_async_copy(others, others, g_rsem.at[sem]).wait()
+            pltpu.make_async_copy(others, others, g_ssem.at[sem]).wait()
+
+        def unpack(out, packed):
+            for k in range(T2):
+                for s in range(NS):
+                    out[k, s * LINES : (s + 1) * LINES] = packed[s, k * LINES : (k + 1) * LINES]
+
+        per = 2 * (X + T1)
+        halo_parts = tuple(
+            ((of[3], 0, T1, S1), (of[4], T1, T1, S1), (of[1], 2 * T1, X, S), (of[2], 2 * T1 + X, X, S)) for of in kept
+        )
+        halo_at = (hb, he)
+
+        def halo_send(f, par):
+            for side, there, dev in ((0, has_lo, lo_dev), (1, has_hi, hi_dev)):
+                @pl.when(there)
+                def _():
+                    for ref, first, count, size in halo_parts[f]:
+                        start_row = HALO if side == 0 else size
+                        pltpu.make_async_remote_copy(
+                            src_ref=ref.at[:, pl.ds(start_row, HALO)],
+                            dst_ref=halo_at[f].at[par, 1 - side, pl.ds(first, count)],
+                            send_sem=h_ssem.at[2 * f + par, side],
+                            recv_sem=h_rsem.at[2 * f + par, 1 - side],
+                            device_id=dev,
+                            device_id_type=MESH,
+                        ).start()
+
+        def halo_wait(view_of, sem):
+            for side, there in ((0, has_lo), (1, has_hi)):
+                @pl.when(there)
+                def _():
+                    view = view_of(side)
+                    pltpu.make_async_copy(view, view, h_rsem.at[sem, side]).wait()
+                    pltpu.make_async_copy(view, view, h_ssem.at[sem, side]).wait()
+
+        chunk = lax.rem(lane(NS * LINES), CHUNK)
+
+        def down2(v):
+            return jnp.where(chunk == 0, roll(roll(v, 1 - CHUNK, 1), 1, 0), roll(v, 1, 1))
+
+        def up2(v):
+            return jnp.where(chunk == CHUNK - 1, roll(roll(v, CHUNK - 1, 1), -1, 0), roll(v, -1, 1))
+
+        def down3(v):
+            return jnp.where(chunk < CHUNK // 2, roll(roll(v, -(CHUNK // 2), 1), 1, 0), roll(v, CHUNK // 2, 1))
+
+        def up3(v):
+            return jnp.where(chunk >= CHUNK // 2, roll(roll(v, CHUNK // 2, 1), -1, 0), roll(v, -(CHUNK // 2), 1))
+
+        def lap_all(w, vs, step, down, up):
+            T = len(vs)
+            out = []
+            for t in range(T):
+                v = vs[t]
+                below = vs[t - 1] if t > 0 else roll(vs[T - 1], GY, 1)
+                above = vs[t + 1] if t < T - 1 else roll(vs[0], -GY, 1)
+                acc = w[F_DG, t] * v - w[F_XM, t] * below - w[F_XP, t] * above
+                acc = acc - w[F_YM, t] * roll(v, step, 1) - w[F_YP, t] * roll(v, -step, 1)
+                out.append(acc - w[F_ZM, t] * down(v) - w[F_ZP, t] * up(v))
+            return out
+
+        def complete_all(w, step, up):
+            T = w.shape[1]
+            for t in range(T):
+                w[F_INV, t] = 1.0 / w[F_DG, t]
+                w[F_XP, t] = w[F_XM, t + 1] if t < T - 1 else roll(w[F_XM, 0], -GY, 1)
+                w[F_YP, t] = roll(w[F_YM, t], -step, 1)
+                w[F_ZP, t] = up(w[F_ZM, t])
+
+        def world():
+            def apply2(v):
+                return lap_all(w2, v, CHUNK, down2, up2)
+
+            def apply3(v):
+                return lap_all(w3, v, 2 * CHUNK, down3, up3)
+
+            def scaled(w, r):
+                return [w[F_INV, t] * r[t] for t in range(len(r))]
+
+            def minus(a, b):
+                return [x - y for x, y in zip(a, b)]
+
+            def plus(*many):
+                return [sum(vs[1:], vs[0]) for vs in zip(*many)]
+
+            def first(w, r):
+                return [d * (1.0 / MID) for d in scaled(w, r)]
+
+            def follow(w, u, r, one, two):
+                return [one * a + two * d for a, d in zip(u, scaled(w, r))]
+
+            r = [cres[k] for k in range(T2)]
+            u = first(w2, r)
+            r = minus(r, apply2(u))
+            u2 = follow(w2, u, r, C_ONE, C_TWO)
+            total = plus(u, u2)
+            r = minus(r, apply2(u2))
+            rc = [pair(pair(r[0] + r[1], CHUNK), 1)]
+            u = first(w3, rc)
+            rc = minus(rc, apply3(u))
+            v = follow(w3, u, rc, C_ONE, C_TWO)
+            e = plus(u, v)
+            rc = minus(rc, apply3(v))
+            e = plus(e, follow(w3, v, rc, C_THREE, C_FOUR))
+            e = [e[0]] * T2
+            total = plus(total, e)
+            r = minus(r, apply2(e))
+            u = first(w2, r)
+            r = minus(r, apply2(u))
+            total = plus(total, u, follow(w2, u, r, C_ONE, C_TWO))
+            for k in range(T2):
+                e2[k, HALO : HALO + NS * LINES] = total[k]
+
+        def precondition():
+            world()
+            own = lax.rem(lane(CHUNK), CHUNK) == row(CHUNK)
+            for d in range(LINES + 2):
+                for k in range(T2):
+                    line = e2[k, pl.ds(slab * LINES + HALO - 1 + d, 1)]
+                    v = jnp.where(own, jnp.broadcast_to(line, (CHUNK, LANES)), 0.0)
+                    v = pair(pair(v, 1), 2)
+                    for t in (2 * k, 2 * k + 1):
+                        for half in range(2):
+                            ua[t, pl.ds(HALO + 2 * CHUNK * d + half, CHUNK, stride=2)] = v
+
+            def put1(k, v):
+                for t in (2 * k, 2 * k + 1):
+                    for half in range(2):
+                        va[t, pl.ds(half, W1, stride=2)] = v
+
+            after(w1, ua, ub, rr1, s1, r1, put1, 2)
+
+            def put0(t, v):
+                vz[t, HALO : HALO + W] = v
+
+            after(w0, va, vb, rr, s0, r0, put0, 1)
+
+        def total_of(v):
+            return jnp.sum(jnp.sum(v, axis=0, keepdims=True), axis=1, keepdims=True)
+
+        lane_1 = lane(1)
+
+        def image_and_dots(par):
+            rz = zaz = zq = None
+            own = slice(HALO, HALO + S)
+            for t in range(X):
+                image = lap(w0, vz, t, 1)
+                az[t] = image
+                z = vz[t, 2 * HALO : 2 * HALO + S]
+                parts = (r_ref[t, own] * z, z * image[own], z * q_ref[t, own])
+                if t == 0:
+                    rz, zaz, zq = parts
+                else:
+                    rz, zaz, zq = rz + parts[0], zaz + parts[1], zq + parts[2]
+            msg[par, T2 * LINES :] = jnp.where(
+                lane_1 == 0, total_of(rz), jnp.where(lane_1 == 1, total_of(zaz), total_of(zq))
+            )
+
+        def lane_of(v, i):
+            return jnp.sum(jnp.where(lane_1 == i, v, 0.0), axis=1, keepdims=True)
+
+        def scalars(par, rz_old, pq_old):
+            sums = gath[par, 0, T2 * LINES :]
+            for s in range(1, NS):
+                sums = sums + gath[par, s, T2 * LINES :]
+            rz, zaz, zq = lane_of(sums, 0), lane_of(sums, 1), lane_of(sums, 2)
+            beta = rz / rz_old
+            pq = zaz + 2.0 * beta * zq + beta * beta * pq_old
+            return rz, pq, rz / pq, beta
+
+        def advance(a, beta):
+            for t in range(X):
+                p = vz[t, HALO : HALO + HALO + S] + beta * p_ref[t]
+                p_ref[t] = p
+                dir_ref[t] = dir_ref[t] + a * p
+                q = az[t] + beta * q_ref[t]
+                q_ref[t] = q
+                r_ref[t] = r_ref[t] - a * q
+
+        def coarse_advance(par, a, beta, fresh):
+            unpack(cnew, gath.at[par])
+            if fresh:
+                unpack(cres, egath.at[par])
+            for k in range(T2):
+                v = cnew[k] + beta * cq[k]
+                cq[k] = v
+                cres[k] = cres[k] - a * v
+
+        def kept_advance(par, a, beta, fresh):
+            for i, (keep, slope) in enumerate(((s1, sq1), (r1, rq1), (s0, sq), (r0, rq))):
+                moved, first, count, size = halo_parts[0][i]
+                true = halo_parts[1][i][0]
+                for t in range(count):
+                    for side, rows in ((0, slice(0, HALO)), (None, slice(HALO, HALO + size)), (1, slice(HALO + size, 2 * HALO + size))):
+                        got = moved[t, rows] if side is None else hb[par, side, first + t]
+                        if a is None:
+                            keep[t, rows] = got
+                            continue
+                        v = got + beta * slope[t, rows]
+                        slope[t, rows] = v
+                        if not fresh:
+                            start = keep[t, rows]
+                        else:
+                            start = true[t, rows] if side is None else he[par, side, first + t]
+                        keep[t, rows] = start - a * v
+
+        for s in range(NS):
+            @pl.when(slab != s)
+            def _():
+                pltpu.make_async_remote_copy(
+                    src_ref=wmsg, dst_ref=wgath.at[pl.ds(pl.multiple_of(slab * WROWS, HALO), WROWS)],
+                    send_sem=g_ssem.at[4], recv_sem=g_rsem.at[4], device_id=device_of(s), device_id_type=MESH,
+                ).start()
+        wgath[pl.ds(pl.multiple_of(slab * WROWS, HALO), WROWS)] = wmsg[...]
+        for side, there, dev in ((0, has_lo, lo_dev), (1, has_hi, hi_dev)):
+            @pl.when(there)
+            def _():
+                pltpu.make_async_remote_copy(
+                    src_ref=w1.at[pl.ds(0, 4), :, pl.ds(HALO if side == 0 else S1, HALO)], dst_ref=sh.at[1 - side],
+                    send_sem=h_ssem.at[4, side], recv_sem=h_rsem.at[4, 1 - side],
+                    device_id=dev, device_id_type=MESH,
+                ).start()
+        presmooth(0, msg, 0)
+        msg[0, T2 * LINES :] = jnp.zeros((1, LANES), f32)
+        to_workers(msg.at[0], gath.at[0], 0)
+        halo_send(0, 0)
+        wait_sent()
+
+        others = wgath.at[pl.ds(0, (NS - 1) * WROWS)]
+        pltpu.make_async_copy(others, others, g_rsem.at[4]).wait()
+        pltpu.make_async_copy(others, others, g_ssem.at[4]).wait()
+        for field in range(4):
+            for k in range(T2):
+                for h in range(LINES):
+                    line = (field * T2 + k) * LINES + h
+                    w2[field, k, pl.ds(h, NS, stride=LINES)] = wgath[pl.ds(line, NS, stride=WROWS)]
+        complete_all(w2, CHUNK, up2)
+        dg, xm, ym, zm = F_DG, F_XM, F_YM, F_ZM
+        ym_all = pair(w2[ym, 0] + w2[ym, 1], 1)
+        zm_all = pair(w2[zm, 0] + w2[zm, 1], CHUNK)
+        between = pair(pair(w2[xm, 1], CHUNK), 1) + pick_high(ym_all, CHUNK) + pick_high(zm_all, 1)
+        w3[dg, 0] = pair(pair(w2[dg, 0] + w2[dg, 1], CHUNK), 1) - 2.0 * between
+        w3[xm, 0] = pair(pair(w2[xm, 0], CHUNK), 1)
+        w3[ym, 0] = pick_low(ym_all, CHUNK)
+        w3[zm, 0] = pick_low(zm_all, 1)
+        complete_all(w3, 2 * CHUNK, up3)
+        halo_wait(lambda side: sh.at[side], 4)
+        for side, there in ((0, has_lo), (1, has_hi)):
+            @pl.when(there)
+            def _():
+                first = 0 if side == 0 else HALO + S1
+                for field in range(4):
+                    w1[field, :, first : first + HALO] = sh[side, field]
+        complete1()
+        from_workers(gath.at[0], 0)
+        unpack(cres, gath.at[0])
+        halo_wait(lambda side: hb.at[0, side], 0)
+        kept_advance(0, None, None, False)
+
+        def step(par, fresh, carry):
+            if fresh:
+                presmooth(1, early, par)
+                to_workers(early.at[par], egath.at[par], 2 + par)
+                halo_send(1, par)
+            precondition()
+            image_and_dots(par)
+            presmooth(0, msg, par)
+            to_workers(msg.at[par], gath.at[par], par)
+            halo_send(0, par)
+            from_workers(gath.at[par], par)
+            rz, pq, a, beta = scalars(par, *carry)
+            if fresh:
+                from_workers(egath.at[par], 2 + par)
+            coarse_advance(par, a, beta, fresh)
+            advance(a, beta)
+            halo_wait(lambda side: hb.at[par, side], par)
+            if fresh:
+                halo_wait(lambda side: he.at[par, side], 2 + par)
+            kept_advance(par, a, beta, fresh)
+            return rz, pq
+
+        carry = step(1, False, (jnp.ones((1, 1), f32), jnp.zeros((1, 1), f32)))
+        carry = lax.fori_loop(1, ITERS - 1, lambda i, c: step(lax.rem(i + 1, 2), True, c), carry)
+        last = ITERS % 2
+        precondition()
+        image_and_dots(last)
+        to_workers(msg.at[last], gath.at[last], last)
+        from_workers(gath.at[last], last)
+        _, _, a, beta = scalars(last, *carry)
+        advance(a, beta)
+
+        for which in range(2):
+            for at in range(0, S, HALO):
+                ref = r_ref if which else dir_ref
+                tiles = block_transpose([ref[t, HALO + at : 2 * HALO + at] for t in range(X)])
+                for t in range(X):
+                    outs[which, t, at : at + HALO] = tiles[t]
+            for t in range(P):
+                remote = jnp.logical_or(block != iz, own_tile != t)
+
+                @pl.when(remote)
+                def _():
+                    back_copy(which, t).start()
+            back_here(which)
+
+        def energy(g):
+            square = 1.0 + g * g
+            return (square * jnp.sqrt(square) - 1.0) * (1.0 / 3.0)
+
+        lanes = lane(S)
+        y_at = lax.rem(lanes, GY)
+        x_first, x_last, y_first = lanes < GY, lanes >= LANES - GY, y_at == 0
+        ends = jnp.where(y_at == GY - 1, 1.0, 0.0) + jnp.where(slab * S + row(S) == NZ - 1, 1.0, 0.0)
+        ends_x = ends + jnp.where(x_last, 1.0, 0.0)
+        fetch = lax.rem(lane_1, GY)
+        packed = jnp.zeros((1, LANES), f32)
+        for k in range(TRIALS):
+            s = jnp.exp2(-jnp.full((1, LANES), tp_ref[k], jnp.int32).astype(f32))
+
+            def trial(t, shift):
+                first = 2 * HALO - shift
+                return f_it[t, first : first + S] + s * dir_ref[t, HALO - shift : HALO - shift + S]
+
+            below = jnp.where(x_first, 0.0, roll(trial(X - 1, 0), GY, 1))
+            for t in range(X):
+                v = trial(t, 0)
+                e = energy(v - below) + energy(v - trial(t, 1))
+                e = e + energy(v - jnp.where(y_first, 0.0, roll(v, 1, 1)))
+                e = e + energy(v) * (ends_x if t == X - 1 else ends)
+                e = e + (0.5 * f_rea[t, HALO : HALO + S] * v - f_src[t, HALO : HALO + S]) * v
+                column = jnp.sum(e, axis=0, keepdims=True)
+                step = 1
+                while step < GY:
+                    column = pair(column, step)
+                    step *= 2
+                packed = packed + jnp.where(fetch == k * X + t, column, 0.0)
+                below = v
+        enmsg[...] = packed
+        engath[slab] = packed
+        for other in range(nx * ny * nz):
+            @pl.when(me != other)
+            def _():
+                energy_copy((other // (ny * nz), other // nz % ny, other % nz)).start()
+        for which in range(2):
+            for t in range(P):
+                @pl.when(jnp.logical_or(block != iz, own_tile != t))
+                def _():
+                    back_copy(which, t).wait_send()
+
+    @pl.when(jnp.logical_not(works))
+    def _():
+        wait_sent()
+
+    for which, out in ((0, dir_out), (1, rem_out)):
+        for own in range(2):
+            @pl.when(jnp.where(block == iz, 1, 0) == own)
+            def _():
+                view = back.at[which, pl.ds(0, Z - own * S)]
+                pltpu.make_async_copy(view, view, b_rsem.at[which]).wait()
+        out[...] = back[which].T.reshape(X, Y, Z)
+    @pl.when(works)
+    def _():
+        others = engath.at[pl.ds(0, NS - 1)]
+        pltpu.make_async_copy(others, others, g_rsem.at[5]).wait()
+        for other in range(nx * ny * nz):
+            @pl.when(me != other)
+            def _():
+                energy_copy((other // (ny * nz), other // nz % ny, other % nz)).wait_send()
+
+    @pl.when(jnp.logical_not(works))
+    def _():
+        pltpu.make_async_copy(engath, engath, g_rsem.at[5]).wait()
+
+    lane_1 = lane(1)
+    fetch = lax.rem(lane_1, GY)
+    layers = jnp.sum(engath[...], axis=0) / (GY * NZ)
+    here = jnp.where(lane_1 // GY == ix, layers, 0.0)
+    at_k = lax.broadcasted_iota(jnp.int32, (TRIALS * X, LANES), 0)
+    mine = jnp.sum(jnp.where(lax.rem(lane(TRIALS * X), GY) == at_k, here, 0.0), axis=1, keepdims=True)
+    mine = jnp.where(lane(TRIALS * X) == lax.rem(at_k, X), mine, 0.0)
+    for k in range(TRIALS):
+        le_ref[k : k + 1] = jnp.sum(mine[k * X : k * X + X], axis=0, keepdims=True)[:, :X]
+        total = jnp.sum(jnp.where(fetch // X == k, layers, 0.0), axis=1, keepdims=True) / (X * nx)
+        en_ref[k : k + 1] = jnp.broadcast_to(total, (1, LANES))
+
+
+def slab_on_device(counts, iterate, source, reaction, trial_powers):
+    X, Y, Z = iterate.shape
+    nx, ny, nz = counts
+    P = nx * ny
+    NS = PLANES * ny * nz
+    S = nz * Z // NS
+    BLOCK = Z // S
+    W, W1 = S + 2 * HALO, S // 2 + 2 * HALO
+    T1, T2, T3 = X // 2, X // 4, X // 8
+    LINES = S // (4 * CHUNK)
+    C_ROWS, ROWS = T2 * LINES, NS * LINES
+    f32 = jnp.float32
+
+    def vm(*shape):
+        return pltpu.VMEM(shape, f32)
+
+    def sem(*shape):
+        return pltpu.SemaphoreType.DMA(shape)
+
+    full, padded = (X, W, LANES), (X, W + 2 * HALO, LANES)
+    full1, padded1 = (T1, W1, LANES), (T1, W1 + 2 * HALO, LANES)
+    scratch = [vm(3, Z, LANES), vm(1, P, W + 2 * HALO, LANES), vm(2, P, W, LANES)]
+    scratch += [vm(*padded), vm(*full), vm(*full)]
+    scratch += [vm(8, *full), vm(8, *full1), vm(8, T2, ROWS, LANES), vm(8, T3, ROWS, LANES)]
+    scratch += [vm(*padded)] * 3 + [vm(*full)] * 10
+    scratch += [vm(*padded1)] * 2 + [vm(*full1)] * 10
+    scratch += [vm(T2, ROWS + 2 * HALO, LANES)] + [vm(T2, ROWS, LANES)] * 3
+    scratch += [vm(X, S + HALO, LANES)] * 2 + [vm(*full)] * 2
+    scratch += [vm(2, C_ROWS + 1, LANES), vm(2, NS, C_ROWS + 1, LANES), vm(2, C_ROWS, LANES), vm(2, NS, C_ROWS, LANES)]
+    scratch += [vm(4 * C_ROWS, LANES), vm(NS * 4 * C_ROWS, LANES)]
+    scratch += [vm(2, 2, 2 * (X + T1), HALO, LANES)] * 2 + [vm(2, 4, T1, HALO, LANES)]
+    scratch += [vm(1, LANES), vm(NS, 1, LANES), vm(2, P, S, LANES), vm(2, Z, LANES)]
+    scratch += [sem(2, BLOCK + 2), sem(2, 3), sem(6), sem(6), sem(5, 2), sem(5, 2), sem(2, P), sem(2), sem(nx * ny * nz)]
+    whole = pl.BlockSpec(memory_space=pltpu.VMEM)
+    out = pl.pallas_call(
+        functools.partial(slab_kernel, (X, Y, Z), counts),
+        out_shape=[
+            jax.ShapeDtypeStruct((X, Y, Z), f32),
+            jax.ShapeDtypeStruct((X, Y, Z), f32),
+            jax.ShapeDtypeStruct((TRIALS, X), f32),
+            jax.ShapeDtypeStruct((TRIALS, LANES), f32),
+        ],
+        in_specs=[pl.BlockSpec(memory_space=pltpu.SMEM), whole, whole, whole],
+        out_specs=[whole] * 4,
+        scratch_shapes=scratch,
+        compiler_params=pltpu.CompilerParams(has_side_effects=True, vmem_limit_bytes=48 * 1024 * 1024),
+        name="newton_step",
+    )(trial_powers, iterate, source, reaction)
+    return out[0], out[1], out[2], out[3][:, 0]
+
+
 def solution(mesh):
     counts = tuple(mesh.shape[axis] for axis in ("gx", "gy", "gz"))
     grid = P("gx", "gy", "gz")
+
+    def on_each(iterate, source, reaction, trial_powers):
+        form = slab_on_device if slab_fits(counts, iterate.shape) else on_device
+        return form(counts, iterate, source, reaction, trial_powers)
+
     return jax.shard_map(
-        functools.partial(on_device, counts),
+        on_each,
         mesh=mesh,
         in_specs=(grid, grid, grid, P()),
         out_specs=(grid, grid, P(None, "gx"), P()),

time: 176 us -> 67 us (0.38)
  Pallas kernels: 170 us -> 60.4 us
    pallas_call x1, Pallas kernels: 170 us -> 60.4 us  [slab_on_device(): pl.pallas_call(functools.partial(slab_kernel, (X, Y, Z), counts), out_sha...]
where the time goes in v2:
time: 67 us; the launch traced here: 66.7 us
  Pallas kernels  60.4 us (90%)
  local copies, waits for them, and re-layouts  5.63 us (8%)
    pallas_call x1, Pallas kernels, slab_on_device(): pl.pallas_call(functools.partial(slab_kernel, (X, Y, Z), counts), out_sha...  60.4 us
    unnamed x11, local copies, waits for them, and re-layouts  5 us

profile of v2, /device:TPU:0, one launch (start us, length us, event | category | flops | bytes accessed | tf_op | source)
XLA Modules:
  0.0 66.7 jit_solution(16049146685213062526)
XLA Ops:
  0.6 0.0 copy-start
  0.6 0.8 %copy-done = f32[8,16,128]{2,1,0:T(8,128)S(1)} copy-done((f32[8,16,128]{2,1,0:T(8,128)S(1)}, f32[8,16,128]{2,1,0:T(8,128)}, u32[]{:S(2)}) %copy-start) | copy-done | bytes 65560
  1.5 0.0 copy-start.1
  1.5 0.8 %copy-done.1 = f32[8,16,128]{2,1,0:T(8,128)S(1)} copy-done((f32[8,16,128]{2,1,0:T(8,128)S(1)}, f32[8,16,128]{2,1,0:T(8,128)}, u32[]{:S(2)}) %copy-start.1) | copy-done | bytes 65560
  2.3 0.0 copy-start.2
  2.3 0.8 %copy-done.2 = f32[8,16,128]{2,1,0:T(8,128)S(1)} copy-done((f32[8,16,128]{2,1,0:T(8,128)S(1)}, f32[8,16,128]{2,1,0:T(8,128)}, u32[]{:S(2)}) %copy-start.2) | copy-done | bytes 65560
  3.2 0.0 copy-start.3
  3.2 0.7 copy-done.3
  3.8 60.4 %newton_step.1 = (f32[8,16,128]{2,1,0:T(8,128)S(1)}, f32[8,16,128]{2,1,0:T(8,128)S(1)}, f32[4,8]{1,0:T(4,128)S(1)}, f32[4,128]{1,0:T(4,128)S(1)}) custom-call(s32[4]{0:T(128)S(1)} %copy-done.3, f32[8,16,128]{2,1,0:T(8,128)S(1)} %copy-done, f32[8,16,128]{2,1,0:T(8,128)S(1)} %copy-done.1, f32[8,16,128]{2,1,0:T(8,128)S(1)} %copy-done.2), custom_call_target="tpu_custom_call" | custom-call | tf_op jit(solution)/shard_map/newton_step/pallas_call | solution.py:1354
  64.2 0.6 slice_reduce_fusion
  64.9 0.6 copy.11
  65.5 0.6 copy.12
  66.1 0.6 copy.13
Async XLA Ops:
  0.6 0.8 %copy-start = (f32[8,16,128]{2,1,0:T(8,128)S(1)}, f32[8,16,128]{2,1,0:T(8,128)}, u32[]{:S(2)}) copy-start(f32[8,16,128]{2,1,0:T(8,128)} %it_in.1) | copy-start | bytes 196612
  1.5 0.8 %copy-start.1 = (f32[8,16,128]{2,1,0:T(8,128)S(1)}, f32[8,16,128]{2,1,0:T(8,128)}, u32[]{:S(2)}) copy-start(f32[8,16,128]{2,1,0:T(8,128)} %src_in.1) | copy-start | bytes 196612
  2.3 0.8 %copy-start.2 = (f32[8,16,128]{2,1,0:T(8,128)S(1)}, f32[8,16,128]{2,1,0:T(8,128)}, u32[]{:S(2)}) copy-start(f32[8,16,128]{2,1,0:T(8,128)} %rea_in.1) | copy-start | bytes 196612
  3.2 0.7 copy-start.3

commit v3 on v2

--- a/solution.py
+++ b/solution.py
@@ -559,7 +559,7 @@
 
 
 def slab_kernel(
-    sizes, counts, tp_ref, it_in, src_in, rea_in, dir_out, rem_out, le_ref, en_ref,
+    sizes, counts, tp_ref, given, fields_out, sums_out,
     turned, d_it, d_rs, f_it, f_rea, f_src, w0, w1, w2, w3,
     va, vb, vz, rr, az, sa, ra, sb, rb, s0, r0, sq, rq,
     ua, ub, r1in, rr1, sa1, ra1, sb1, rb1, s1, r1, sq1, rq1, e2, cres, cq, cnew,
@@ -665,6 +665,28 @@
     def both(a, b):
         return b if a is None else jnp.logical_and(a, b)
 
+    barrier = pltpu.get_barrier_semaphore()
+    for other in range(nx * ny * nz):
+        @pl.when(me != other)
+        def _():
+            pl.semaphore_signal(
+                barrier, inc=1, device_id=(other // (ny * nz), other // nz % ny, other % nz), device_id_type=MESH
+            )
+
+    for a, (which, landed, halo) in enumerate(parts):
+        for i in (0,) if a == 0 else (1, 2):
+            turned[i] = given[i * LANES : (i + 1) * LANES].T
+        if a == 0:
+            pl.semaphore_wait(barrier, nx * ny * nz - 1)
+        for to, exists, first, count, there, number in pieces(a):
+            @pl.when(both(exists, to != slab))
+            def _():
+                piece(a, to, first, count, there, number).start()
+
+            @pl.when(both(exists, to == slab))
+            def _():
+                landed[:, own_tile, there : there + count] = turned[which, first : first + count]
+
     @pl.when(works)
     def _():
         for ref in (va, vb, vz, ua, ub, r1in, e2, p_ref, dir_ref, q_ref, sq, rq, sq1, rq1, cq, w1):
@@ -676,18 +698,6 @@
                 for ref in (hb, he):
                     ref[:, side] = jnp.zeros(ref.shape[:1] + ref.shape[2:], f32)
 
-    for a, (which, landed, halo) in enumerate(parts):
-        for i, given in ((0, it_in),) if a == 0 else ((1, rea_in), (2, src_in)):
-            turned[i] = given[...].reshape(LANES, Z).T
-        for to, exists, first, count, there, number in pieces(a):
-            @pl.when(both(exists, to != slab))
-            def _():
-                piece(a, to, first, count, there, number).start()
-
-            @pl.when(both(exists, to == slab))
-            def _():
-                landed[:, own_tile, there : there + count] = turned[which, first : first + count]
-
     def wait_sent():
         for a in range(2):
             for to, exists, first, count, there, number in pieces(a):
@@ -703,8 +713,8 @@
                 view = parts[a][1].at[:, pl.ds(0, P - own), pl.ds(first, count)]
                 pltpu.make_async_copy(view, view, d_rsem.at[a, kind]).wait()
 
-    def gather_block():
-        for a, (_, landed, halo) in enumerate(parts):
+    def gather_block(a):
+        for _, landed, halo in parts[a : a + 1]:
             @pl.when(slab == 0)
             def _():
                 landed[:, :, :halo] = jnp.zeros((landed.shape[0], P, halo, LANES), f32)
@@ -750,7 +760,7 @@
 
     @pl.when(works)
     def _():
-        gather_block()
+        gather_block(0)
 
         lanes = lane(W)
         z_at = slab * S + row(W) - HALO
@@ -763,14 +773,14 @@
 
         def face(g):
             square = g * g
-            root = jnp.sqrt(1.0 + square)
-            return (1.0 + 2.0 * square) / root, g * root
+            one = 1.0 + square
+            inverse = lax.rsqrt(one)
+            return (one + square) * inverse, g * (one * inverse)
 
         def window(t):
             return f_it[t, HALO : HALO + W]
 
         low_w, low_p = face(window(0) - jnp.where(x_first, 0.0, roll(window(X - 1), GY, 1)))
-        first_w = low_w
         for t in range(X):
             c = window(t)
             beyond = window(t + 1) if t < X - 1 else jnp.where(x_last, 0.0, roll(window(0), -GY, 1))
@@ -779,21 +789,25 @@
             yh_w, yh_p = face(jnp.where(y_last, 0.0, roll(c, -1, 1)) - c)
             zl_w, zl_p = face(c - f_it[t, HALO - 1 : HALO - 1 + W])
             zh_w, zh_p = face(f_it[t, HALO + 1 : HALO + 1 + W] - c)
-            rea = f_rea[t]
-            diagonal = rea + low_w + high_w + yl_w + yh_w + zl_w + zh_w
-            w0[F_DG, t] = diagonal
-            w0[F_INV, t] = 1.0 / diagonal
+            w0[F_DG, t] = low_w + high_w + yl_w + yh_w + zl_w + zh_w
             w0[F_XM, t] = jnp.where(x_first, 0.0, low_w) if t == 0 else low_w
             w0[F_XP, t] = jnp.where(x_last, 0.0, high_w) if t == X - 1 else high_w
             w0[F_YM, t] = jnp.where(y_first, 0.0, yl_w)
             w0[F_YP, t] = jnp.where(y_last, 0.0, yh_w)
             w0[F_ZM, t] = jnp.where(z_low, zl_w, 0.0)
             w0[F_ZP, t] = jnp.where(z_high, zh_w, 0.0)
-            r = f_src[t] - rea * c + (high_p - low_p) + (yh_p - yl_p) + (zh_p - zl_p)
-            r = jnp.where(inside, r, 0.0)
+            az[t] = (high_p - low_p) + (yh_p - yl_p) + (zh_p - zl_p)
+            low_w, low_p = high_w, high_p
+
+        gather_block(1)
+        for t in range(X):
+            rea = f_rea[t]
+            diagonal = w0[F_DG, t] + rea
+            w0[F_DG, t] = diagonal
+            w0[F_INV, t] = 1.0 / diagonal
+            r = jnp.where(inside, f_src[t] - rea * window(t) + az[t], 0.0)
             az[t] = r
             r_ref[t] = r
-            low_w, low_p = high_w, high_p
 
         def coarsen(get, step):
             def build(k):
@@ -1238,7 +1252,7 @@
 
         def energy(g):
             square = 1.0 + g * g
-            return (square * jnp.sqrt(square) - 1.0) * (1.0 / 3.0)
+            return (square * (square * lax.rsqrt(square)) - 1.0) * (1.0 / 3.0)
 
         lanes = lane(S)
         y_at = lax.rem(lanes, GY)
@@ -1284,13 +1298,13 @@
     def _():
         wait_sent()
 
-    for which, out in ((0, dir_out), (1, rem_out)):
+    for which in range(2):
         for own in range(2):
             @pl.when(jnp.where(block == iz, 1, 0) == own)
             def _():
                 view = back.at[which, pl.ds(0, Z - own * S)]
                 pltpu.make_async_copy(view, view, b_rsem.at[which]).wait()
-        out[...] = back[which].T.reshape(X, Y, Z)
+        fields_out[which] = back[which].T.reshape(X, Y, Z)
     @pl.when(works)
     def _():
         others = engath.at[pl.ds(0, NS - 1)]
@@ -1312,9 +1326,23 @@
     mine = jnp.sum(jnp.where(lax.rem(lane(TRIALS * X), GY) == at_k, here, 0.0), axis=1, keepdims=True)
     mine = jnp.where(lane(TRIALS * X) == lax.rem(at_k, X), mine, 0.0)
     for k in range(TRIALS):
-        le_ref[k : k + 1] = jnp.sum(mine[k * X : k * X + X], axis=0, keepdims=True)[:, :X]
+        sums_out[k : k + 1] = jnp.sum(mine[k * X : k * X + X], axis=0, keepdims=True)
         total = jnp.sum(jnp.where(fetch // X == k, layers, 0.0), axis=1, keepdims=True) / (X * nx)
-        en_ref[k : k + 1] = jnp.broadcast_to(total, (1, LANES))
+        sums_out[TRIALS + k : TRIALS + k + 1] = jnp.broadcast_to(total, (1, LANES))
+
+
+def hand_out(fields, sums, dir_out, rem_out, le_out, en_out, le, en, sem):
+    copies = [pltpu.make_async_copy(fields.at[i], out, sem.at[i]) for i, out in ((0, dir_out), (1, rem_out))]
+    for copy in copies:
+        copy.start()
+    le[...] = sums[:TRIALS, : le.shape[1]]
+    for k in range(TRIALS):
+        en[k] = jnp.max(sums[TRIALS + k : TRIALS + k + 1])
+    copies += [pltpu.make_async_copy(le, le_out, sem.at[2]), pltpu.make_async_copy(en, en_out, sem.at[3])]
+    for copy in copies[2:]:
+        copy.start()
+    for copy in copies:
+        copy.wait()
 
 
 def slab_on_device(counts, iterate, source, reaction, trial_powers):
@@ -1351,21 +1379,32 @@
     scratch += [vm(1, LANES), vm(NS, 1, LANES), vm(2, P, S, LANES), vm(2, Z, LANES)]
     scratch += [sem(2, BLOCK + 2), sem(2, 3), sem(6), sem(6), sem(5, 2), sem(5, 2), sem(2, P), sem(2), sem(nx * ny * nz)]
     whole = pl.BlockSpec(memory_space=pltpu.VMEM)
-    out = pl.pallas_call(
+    given = jnp.concatenate([v.reshape(LANES, Z) for v in (iterate, reaction, source)])
+    fields, sums = pl.pallas_call(
         functools.partial(slab_kernel, (X, Y, Z), counts),
+        out_shape=[jax.ShapeDtypeStruct((2, X, Y, Z), f32), jax.ShapeDtypeStruct((2 * TRIALS, LANES), f32)],
+        in_specs=[pl.BlockSpec(memory_space=pltpu.SMEM), whole],
+        out_specs=[whole] * 2,
+        scratch_shapes=scratch,
+        compiler_params=pltpu.CompilerParams(
+            has_side_effects=True, collective_id=0, vmem_limit_bytes=32 * 1024 * 1024
+        ),
+        name="newton_step",
+    )(trial_powers, given)
+    return pl.pallas_call(
+        hand_out,
         out_shape=[
             jax.ShapeDtypeStruct((X, Y, Z), f32),
             jax.ShapeDtypeStruct((X, Y, Z), f32),
             jax.ShapeDtypeStruct((TRIALS, X), f32),
-            jax.ShapeDtypeStruct((TRIALS, LANES), f32),
+            jax.ShapeDtypeStruct((TRIALS,), f32),
         ],
-        in_specs=[pl.BlockSpec(memory_space=pltpu.SMEM), whole, whole, whole],
-        out_specs=[whole] * 4,
-        scratch_shapes=scratch,
-        compiler_params=pltpu.CompilerParams(has_side_effects=True, vmem_limit_bytes=48 * 1024 * 1024),
-        name="newton_step",
-    )(trial_powers, iterate, source, reaction)
-    return out[0], out[1], out[2], out[3][:, 0]
+        in_specs=[whole] * 2,
+        out_specs=[pl.BlockSpec(memory_space=pl.ANY)] * 4,
+        scratch_shapes=[vm(TRIALS, X), pltpu.SMEM((TRIALS,), f32), sem(4)],
+        compiler_params=pltpu.CompilerParams(vmem_limit_bytes=32 * 1024 * 1024),
+        name="hand_out",
+    )(fields, sums)
 
 
 def solution(mesh):

time: 67 us -> 59.6 us (0.89)
  local copies, waits for them, and re-layouts: 5.63 us -> 0.01 us
  Pallas kernels: 60.4 us -> 57.9 us
  other arithmetic: 0 us -> 0.92 us
    unnamed x11 -> x2, local copies, waits for them, and re-layouts: 5 us -> 0.01 us
    pallas_call x1, Pallas kernels: 60.4 us -> 57.2 us  [slab_on_device(): pl.pallas_call(functools.partial(slab_kernel, (X, Y, Z), counts), out_sha...]
    concatenate x0 -> x1, other arithmetic: none -> 0.92 us  [slab_on_device(): jnp.concatenate([v.reshape(LANES, Z) for v in (iterate, reaction, source)])]
    pallas_call x0 -> x1, Pallas kernels: none -> 0.7 us  [slab_on_device(): pl.pallas_call(hand_out, out_shape=[jax.ShapeDtypeStruct((X, Y, Z), f32),...]
where the time goes in v3:
time: 59.6 us; the launch traced here: 59.5 us
  Pallas kernels  57.9 us (97%)
  other arithmetic  0.92 us (2%)
  between operations  0.66 us (1%)
    pallas_call x1, Pallas kernels, slab_on_device(): pl.pallas_call(functools.partial(slab_kernel, (X, Y, Z), counts), out_sha...  57.2 us

profile of v3, /device:TPU:0, one launch (start us, length us, event | category | flops | bytes accessed | tf_op | source)
XLA Modules:
  0.0 59.5 jit_solution(2509420901173501587)
XLA Ops:
  0.6 0.0 copy-start
  0.6 0.9 %pad_maximum_fusion.given = f32[384,128]{1,0:T(8,128)S(1)} fusion(f32[128,128]{1,0:T(8,128)} %bitcast.3, f32[128,128]{1,0:T(8,128)} %bitcast.4, f32[128,128]{1,0:T(8,128)} %bitcast.5), kind=kLoop, calls=%fused_computation | loop fusion | flops 98304 | bytes 393216 | tf_op jit(solution)/shard_map/concatenate | solution.py:1382
  1.6 0.0 copy-done
  1.6 57.2 %newton_step.1 = (f32[2,8,16,128]{3,2,1,0:T(8,128)S(1)}, f32[8,128]{1,0:T(8,128)S(1)}) custom-call(s32[4]{0:T(128)S(1)} %copy-done, f32[384,128]{1,0:T(8,128)S(1)} %pad_maximum_fusion.given), custom_call_target="tpu_custom_call" | custom-call | tf_op jit(solution)/shard_map/newton_step/pallas_call | solution.py:1383
  58.8 0.7 %hand_out.1 = (f32[8,16,128]{2,1,0:T(8,128)}, f32[8,16,128]{2,1,0:T(8,128)}, f32[4,8]{1,0:T(4,128)}, f32[4]{0:T(128)}) custom-call(f32[2,8,16,128]{3,2,1,0:T(8,128)S(1)} %get-tuple-element.6.fields, f32[8,128]{1,0:T(8,128)S(1)} %get-tuple-element.7.sums), custom_call_target="tpu_custom_call" | custom-call | tf_op jit(solution)/shard_map/hand_out/pallas_call | solution.py:1394
Async XLA Ops:
  0.6 0.9 %copy-start = (s32[4]{0:T(128)S(1)}, s32[4]{0:T(128)}, u32[]{:S(2)}) copy-start(s32[4]{0:T(128)} %tp_ref.1) | copy-start | bytes 52

commit v4 on v3

--- a/solution.py
+++ b/solution.py
@@ -561,11 +561,11 @@
 def slab_kernel(
     sizes, counts, tp_ref, given, fields_out, sums_out,
     turned, d_it, d_rs, f_it, f_rea, f_src, w0, w1, w2, w3,
-    va, vb, vz, rr, az, sa, ra, sb, rb, s0, r0, sq, rq,
-    ua, ub, r1in, rr1, sa1, ra1, sb1, rb1, s1, r1, sq1, rq1, e2, cres, cq, cnew,
+    va, vb, vz, rr, az, sa, ra, sb, rb, sc, rc, s0, r0, sq, rq,
+    ua, ub, r1in, rr1, sa1, ra1, sb1, rb1, sc1, rc1, s1, r1, sq1, rq1, e2, cres, cq, cnew,
     p_ref, dir_ref, q_ref, r_ref,
     msg, gath, early, egath, wmsg, wgath, hb, he, sh, enmsg, engath, outs, back,
-    d_ssem, d_rsem, g_ssem, g_rsem, h_ssem, h_rsem, b_ssem, b_rsem, e_ssem,
+    d_ssem, d_rsem, g_ssem, g_rsem, h_ssem, h_rsem, b_ssem, b_rsem, counted,
 ):
     X, Y, Z = sizes
     nx, ny, nz = counts
@@ -738,7 +738,7 @@
         return pltpu.make_async_remote_copy(
             src_ref=outs.at[which, t],
             dst_ref=back.at[which, pl.ds(pl.multiple_of(S * j, HALO), S)],
-            send_sem=b_ssem.at[which, t],
+            send_sem=b_ssem.at[which],
             recv_sem=b_rsem.at[which],
             device_id=(t // ny, t % ny, block),
             device_id_type=MESH,
@@ -752,7 +752,7 @@
     def energy_copy(dev):
         return pltpu.make_async_remote_copy(
             src_ref=enmsg, dst_ref=engath.at[slab],
-            send_sem=e_ssem.at[(dev[0] * ny + dev[1]) * nz + dev[2]], recv_sem=g_rsem.at[5],
+            send_sem=g_ssem.at[5], recv_sem=g_rsem.at[5],
             device_id=dev, device_id_type=MESH,
         )
 
@@ -864,55 +864,58 @@
             for field, value in zip((F_DG, F_XM, F_YM, F_ZM), coarsen(halves1, 2)(k)):
                 pack(wmsg, (field * T2 + k) * LINES, value)
 
-        def laps(w, vs, t, step):
+        def sweep(w, v, step, use):
             T, n = w.shape[1], w.shape[2]
-            mid = slice(HALO, HALO + n)
-            weights = [w[field, t] for field in range(F_INV)]
-            out = []
-            for v in vs:
-                c = v[t, mid]
-                below = v[t - 1, mid] if t > 0 else roll(v[T - 1, mid], GY, 1)
-                above = v[t + 1, mid] if t < T - 1 else roll(v[0, mid], -GY, 1)
-                acc = weights[F_DG] * c - weights[F_XM] * below - weights[F_XP] * above
-                acc = acc - weights[F_YM] * roll(c, step, 1) - weights[F_YP] * roll(c, -step, 1)
-                acc = acc - weights[F_ZM] * v[t, HALO - 1 : HALO - 1 + n]
-                out.append(acc - weights[F_ZP] * v[t, HALO + 1 : HALO + 1 + n])
-            return out
-
-        def lap(w, v, t, step):
-            return laps(w, [v], t, step)[0]
-
-        def centre(v, t, n):
-            return v[t, HALO : HALO + n]
+            for at in range(0, n, HALO):
+                rows, shifted = slice(at, at + HALO), slice(at + HALO, at + 2 * HALO)
+                c = [v[t, shifted] for t in range(T)]
+                low = w[F_XM, 0, rows]
+                for t in range(T):
+                    below = c[t - 1] if t > 0 else roll(c[T - 1], GY, 1)
+                    above = c[t + 1] if t < T - 1 else roll(c[0], -GY, 1)
+                    high = w[F_XM, t + 1, rows] if t < T - 1 else w[F_XP, t, rows]
+                    ym = w[F_YM, t, rows]
+                    acc = w[F_DG, t, rows] * c[t] - low * below - high * above
+                    acc = acc - ym * roll(c[t], step, 1) - roll(ym * c[t], -step, 1)
+                    acc = acc - w[F_ZM, t, rows] * v[t, at + HALO - 1 : at + 2 * HALO - 1]
+                    acc = acc - w[F_ZP, t, rows] * v[t, at + HALO + 1 : at + 2 * HALO + 1]
+                    use(t, rows, shifted, c[t], acc)
+                    low = high
 
         def before(w, r_of, u1, u2, rem1, s_out, r_out, step):
             T, n = w.shape[1], w.shape[2]
-            mid = slice(HALO, HALO + n)
-            for t in range(T):
-                u1[t, mid] = w[F_INV, t] * r_of[t] * (1.0 / MID)
-            for t in range(T):
-                r = r_of[t] - lap(w, u1, t, step)
-                first = centre(u1, t, n)
-                u = C_ONE * first + C_TWO * w[F_INV, t] * r
-                u2[t, mid] = u
-                s_out[t] = first + u
-                rem1[t] = r
-            for t in range(T):
-                r_out[t] = rem1[t] - lap(w, u2, t, step)
+            for at in range(0, n, HALO):
+                for t in range(T):
+                    rows = slice(at, at + HALO)
+                    u1[t, at + HALO : at + 2 * HALO] = w[F_INV, t, rows] * r_of[t, rows] * (1.0 / MID)
+
+            def second(t, rows, shifted, first, image):
+                r = r_of[t, rows] - image
+                u = C_ONE * first + C_TWO * w[F_INV, t, rows] * r
+                u2[t, shifted] = u
+                s_out[t, rows] = first + u
+                rem1[t, rows] = r
+
+            def rest(t, rows, shifted, u, image):
+                r_out[t, rows] = rem1[t, rows] - image
+
+            sweep(w, u1, step, second)
+            sweep(w, u2, step, rest)
 
         def after(w, e, u1, rem1, s_in, r_in, put, step):
-            T, n = w.shape[1], w.shape[2]
-            mid = slice(HALO, HALO + n)
-            for t in range(T):
-                r = r_in[t] - lap(w, e, t, step)
-                rem1[t] = r
-                u1[t, mid] = w[F_INV, t] * r * (1.0 / MID)
-            for t in range(T):
-                r = rem1[t] - lap(w, u1, t, step)
-                u = centre(u1, t, n)
-                put(t, s_in[t] + centre(e, t, n) + u + (C_ONE * u + C_TWO * w[F_INV, t] * r))
-
-        kept = ((az, sa, ra, sa1, ra1), (r_ref, sb, rb, sb1, rb1))
+            def first(t, rows, shifted, c, image):
+                r = r_in[t, rows] - image
+                rem1[t, rows] = r
+                u1[t, shifted] = w[F_INV, t, rows] * r * (1.0 / MID)
+
+            def second(t, rows, shifted, u, image):
+                r = rem1[t, rows] - image
+                put(t, rows, s_in[t, rows] + e[t, shifted] + (1.0 + C_ONE) * u + C_TWO * w[F_INV, t, rows] * r)
+
+            sweep(w, e, step, first)
+            sweep(w, u1, step, second)
+
+        kept = ((az, sa, ra, sa1, ra1), (r_ref, sb, rb, sb1, rb1), (r_ref, sc, rc, sc1, rc1))
 
         def presmooth(f, ref, par):
             r_of, s_out, r_out, s1_out, r1_out = kept[f]
@@ -955,7 +958,7 @@
         halo_parts = tuple(
             ((of[3], 0, T1, S1), (of[4], T1, T1, S1), (of[1], 2 * T1, X, S), (of[2], 2 * T1 + X, X, S)) for of in kept
         )
-        halo_at = (hb, he)
+        halo_at = (hb, he, he)
 
         def halo_send(f, par):
             for side, there, dev in ((0, has_lo, lo_dev), (1, has_hi, hi_dev)):
@@ -966,8 +969,8 @@
                         pltpu.make_async_remote_copy(
                             src_ref=ref.at[:, pl.ds(start_row, HALO)],
                             dst_ref=halo_at[f].at[par, 1 - side, pl.ds(first, count)],
-                            send_sem=h_ssem.at[2 * f + par, side],
-                            recv_sem=h_rsem.at[2 * f + par, 1 - side],
+                            send_sem=h_ssem.at[2 * min(f, 1) + par, side],
+                            recv_sem=h_rsem.at[2 * min(f, 1) + par, 1 - side],
                             device_id=dev,
                             device_id_type=MESH,
                         ).start()
@@ -1059,7 +1062,6 @@
                 e2[k, HALO : HALO + NS * LINES] = total[k]
 
         def precondition():
-            world()
             own = lax.rem(lane(CHUNK), CHUNK) == row(CHUNK)
             for d in range(LINES + 2):
                 for k in range(T2):
@@ -1070,16 +1072,15 @@
                         for half in range(2):
                             ua[t, pl.ds(HALO + 2 * CHUNK * d + half, CHUNK, stride=2)] = v
 
-            def put1(k, v):
+            def put1(k, rows, v):
                 for t in (2 * k, 2 * k + 1):
                     for half in range(2):
-                        va[t, pl.ds(half, W1, stride=2)] = v
+                        va[t, pl.ds(2 * rows.start + half, HALO, stride=2)] = v
+
+            def put0(t, rows, v):
+                vz[t, rows.start + HALO : rows.stop + HALO] = v
 
             after(w1, ua, ub, rr1, s1, r1, put1, 2)
-
-            def put0(t, v):
-                vz[t, HALO : HALO + W] = v
-
             after(w0, va, vb, rr, s0, r0, put0, 1)
 
         def total_of(v):
@@ -1088,20 +1089,19 @@
         lane_1 = lane(1)
 
         def image_and_dots(par):
-            rz = zaz = zq = None
-            own = slice(HALO, HALO + S)
-            for t in range(X):
-                image = lap(w0, vz, t, 1)
-                az[t] = image
-                z = vz[t, 2 * HALO : 2 * HALO + S]
-                parts = (r_ref[t, own] * z, z * image[own], z * q_ref[t, own])
-                if t == 0:
-                    rz, zaz, zq = parts
-                else:
-                    rz, zaz, zq = rz + parts[0], zaz + parts[1], zq + parts[2]
-            msg[par, T2 * LINES :] = jnp.where(
-                lane_1 == 0, total_of(rz), jnp.where(lane_1 == 1, total_of(zaz), total_of(zq))
-            )
+            sums = []
+
+            def use(t, rows, shifted, z, image):
+                az[t, rows] = image
+                if HALO <= rows.start < HALO + S:
+                    parts = (r_ref[t, rows] * z, z * image, z * q_ref[t, rows])
+                    sums[:] = [a + b for a, b in zip(sums, parts)] if sums else parts
+
+            sweep(w0, vz, 1, use)
+            rz, zaz, zq = (total_of(v) for v in sums)
+            msg[par, T2 * LINES :] = jnp.where(lane_1 == 0, rz, jnp.where(lane_1 == 1, zaz, zq))
+
+        lane_1 = lane(1)
 
         def lane_of(v, i):
             return jnp.sum(jnp.where(lane_1 == i, v, 0.0), axis=1, keepdims=True)
@@ -1136,7 +1136,7 @@
         def kept_advance(par, a, beta, fresh):
             for i, (keep, slope) in enumerate(((s1, sq1), (r1, rq1), (s0, sq), (r0, rq))):
                 moved, first, count, size = halo_parts[0][i]
-                true = halo_parts[1][i][0]
+                true = halo_parts[1 + par][i][0]
                 for t in range(count):
                     for side, rows in ((0, slice(0, HALO)), (None, slice(HALO, HALO + size)), (1, slice(HALO + size, 2 * HALO + size))):
                         got = moved[t, rows] if side is None else hb[par, side, first + t]
@@ -1204,39 +1204,39 @@
         halo_wait(lambda side: hb.at[0, side], 0)
         kept_advance(0, None, None, False)
 
-        def step(par, fresh, carry):
+        rz, pq = jnp.ones((1, 1), f32), jnp.zeros((1, 1), f32)
+        a = beta = None
+        for it in range(ITERS):
+            par, last, first = (it + 1) % 2, it == ITERS - 1, it == 0
+            fresh = not (first or last)
             if fresh:
-                presmooth(1, early, par)
+                presmooth(1 + par, early, par)
+            world()
+            if fresh:
                 to_workers(early.at[par], egath.at[par], 2 + par)
-                halo_send(1, par)
+                halo_send(1 + par, par)
+            if not first:
+                was = it % 2
+                halo_wait(lambda side: hb.at[was, side], was)
+                if it > 1:
+                    halo_wait(lambda side: he.at[was, side], 2 + was)
+                kept_advance(was, a, beta, it > 1)
             precondition()
             image_and_dots(par)
-            presmooth(0, msg, par)
+            if not last:
+                presmooth(0, msg, par)
             to_workers(msg.at[par], gath.at[par], par)
-            halo_send(0, par)
+            if not last:
+                halo_send(0, par)
             from_workers(gath.at[par], par)
-            rz, pq, a, beta = scalars(par, *carry)
+            rz, pq, a, beta = scalars(par, rz, pq)
             if fresh:
                 from_workers(egath.at[par], 2 + par)
-            coarse_advance(par, a, beta, fresh)
+            if not last:
+                coarse_advance(par, a, beta, fresh)
             advance(a, beta)
-            halo_wait(lambda side: hb.at[par, side], par)
-            if fresh:
-                halo_wait(lambda side: he.at[par, side], 2 + par)
-            kept_advance(par, a, beta, fresh)
-            return rz, pq
-
-        carry = step(1, False, (jnp.ones((1, 1), f32), jnp.zeros((1, 1), f32)))
-        carry = lax.fori_loop(1, ITERS - 1, lambda i, c: step(lax.rem(i + 1, 2), True, c), carry)
-        last = ITERS % 2
-        precondition()
-        image_and_dots(last)
-        to_workers(msg.at[last], gath.at[last], last)
-        from_workers(gath.at[last], last)
-        _, _, a, beta = scalars(last, *carry)
-        advance(a, beta)
-
-        for which in range(2):
+
+        def send_back(which):
             for at in range(0, S, HALO):
                 ref = r_ref if which else dir_ref
                 tiles = block_transpose([ref[t, HALO + at : 2 * HALO + at] for t in range(X)])
@@ -1249,6 +1249,8 @@
                 def _():
                     back_copy(which, t).start()
             back_here(which)
+
+        send_back(1)
 
         def energy(g):
             square = 1.0 + g * g
@@ -1288,17 +1290,13 @@
             @pl.when(me != other)
             def _():
                 energy_copy((other // (ny * nz), other // nz % ny, other % nz)).start()
-        for which in range(2):
-            for t in range(P):
-                @pl.when(jnp.logical_or(block != iz, own_tile != t))
-                def _():
-                    back_copy(which, t).wait_send()
+        send_back(0)
 
     @pl.when(jnp.logical_not(works))
     def _():
         wait_sent()
 
-    for which in range(2):
+    for which in (1, 0):
         for own in range(2):
             @pl.when(jnp.where(block == iz, 1, 0) == own)
             def _():
@@ -1309,10 +1307,14 @@
     def _():
         others = engath.at[pl.ds(0, NS - 1)]
         pltpu.make_async_copy(others, others, g_rsem.at[5]).wait()
-        for other in range(nx * ny * nz):
-            @pl.when(me != other)
-            def _():
-                energy_copy((other // (ny * nz), other // nz % ny, other % nz)).wait_send()
+        sent = counted.at[pl.ds(0, nx * ny * nz - 1)]
+        pltpu.make_async_copy(sent, sent, g_ssem.at[5]).wait()
+        for which in range(2):
+            for own in range(2):
+                @pl.when(jnp.where(block == iz, 1, 0) == own)
+                def _():
+                    sent = outs.at[which, pl.ds(0, P - own)]
+                    pltpu.make_async_copy(sent, sent, b_ssem.at[which]).wait()
 
     @pl.when(jnp.logical_not(works))
     def _():
@@ -1369,15 +1371,15 @@
     scratch = [vm(3, Z, LANES), vm(1, P, W + 2 * HALO, LANES), vm(2, P, W, LANES)]
     scratch += [vm(*padded), vm(*full), vm(*full)]
     scratch += [vm(8, *full), vm(8, *full1), vm(8, T2, ROWS, LANES), vm(8, T3, ROWS, LANES)]
-    scratch += [vm(*padded)] * 3 + [vm(*full)] * 10
-    scratch += [vm(*padded1)] * 2 + [vm(*full1)] * 10
+    scratch += [vm(*padded)] * 3 + [vm(*full)] * 12
+    scratch += [vm(*padded1)] * 2 + [vm(*full1)] * 12
     scratch += [vm(T2, ROWS + 2 * HALO, LANES)] + [vm(T2, ROWS, LANES)] * 3
     scratch += [vm(X, S + HALO, LANES)] * 2 + [vm(*full)] * 2
     scratch += [vm(2, C_ROWS + 1, LANES), vm(2, NS, C_ROWS + 1, LANES), vm(2, C_ROWS, LANES), vm(2, NS, C_ROWS, LANES)]
     scratch += [vm(4 * C_ROWS, LANES), vm(NS * 4 * C_ROWS, LANES)]
     scratch += [vm(2, 2, 2 * (X + T1), HALO, LANES)] * 2 + [vm(2, 4, T1, HALO, LANES)]
     scratch += [vm(1, LANES), vm(NS, 1, LANES), vm(2, P, S, LANES), vm(2, Z, LANES)]
-    scratch += [sem(2, BLOCK + 2), sem(2, 3), sem(6), sem(6), sem(5, 2), sem(5, 2), sem(2, P), sem(2), sem(nx * ny * nz)]
+    scratch += [sem(2, BLOCK + 2), sem(2, 3), sem(6), sem(6), sem(5, 2), sem(5, 2), sem(2), sem(2), vm(nx * ny * nz, 1, LANES)]
     whole = pl.BlockSpec(memory_space=pltpu.VMEM)
     given = jnp.concatenate([v.reshape(LANES, Z) for v in (iterate, reaction, source)])
     fields, sums = pl.pallas_call(

time: 59.6 us -> 57.1 us (0.958)
  Pallas kernels: 57.9 us -> 55.4 us
    pallas_call x1, Pallas kernels: 57.2 us -> 54.7 us  [slab_on_device(): pl.pallas_call(functools.partial(slab_kernel, (X, Y, Z), counts), out_sha...]
where the time goes in v4:
time: 57.1 us; the launch traced here: 57 us
  Pallas kernels  55.4 us (97%)
  other arithmetic  0.92 us (2%)
  between operations  0.66 us (1%)
    pallas_call x1, Pallas kernels, slab_on_device(): pl.pallas_call(functools.partial(slab_kernel, (X, Y, Z), counts), out_sha...  54.7 us

profile of v4, /device:TPU:0, one launch (start us, length us, event | category | flops | bytes accessed | tf_op | source)
XLA Modules:
  0.0 57.0 jit_solution(13383954655689447457)
XLA Ops:
  0.6 0.0 copy-start
  0.6 0.9 %pad_maximum_fusion.given = f32[384,128]{1,0:T(8,128)S(1)} fusion(f32[128,128]{1,0:T(8,128)} %bitcast.3, f32[128,128]{1,0:T(8,128)} %bitcast.4, f32[128,128]{1,0:T(8,128)} %bitcast.5), kind=kLoop, calls=%fused_computation | loop fusion | flops 98304 | bytes 393216 | tf_op jit(solution)/shard_map/concatenate | solution.py:1384
  1.6 0.0 copy-done
  1.6 54.7 %newton_step.1 = (f32[2,8,16,128]{3,2,1,0:T(8,128)S(1)}, f32[8,128]{1,0:T(8,128)S(1)}) custom-call(s32[4]{0:T(128)S(1)} %copy-done, f32[384,128]{1,0:T(8,128)S(1)} %pad_maximum_fusion.given), custom_call_target="tpu_custom_call" | custom-call | tf_op jit(solution)/shard_map/newton_step/pallas_call | solution.py:1385
  56.3 0.7 %hand_out.1 = (f32[8,16,128]{2,1,0:T(8,128)}, f32[8,16,128]{2,1,0:T(8,128)}, f32[4,8]{1,0:T(4,128)}, f32[4]{0:T(128)}) custom-call(f32[2,8,16,128]{3,2,1,0:T(8,128)S(1)} %get-tuple-element.6.fields, f32[8,128]{1,0:T(8,128)S(1)} %get-tuple-element.7.sums), custom_call_target="tpu_custom_call" | custom-call | tf_op jit(solution)/shard_map/hand_out/pallas_call | solution.py:1396
Async XLA Ops:
  0.6 0.9 %copy-start = (s32[4]{0:T(128)S(1)}, s32[4]{0:T(128)}, u32[]{:S(2)}) copy-start(s32[4]{0:T(128)} %tp_ref.1) | copy-start | bytes 52

commit v5 on v4

--- a/solution.py
+++ b/solution.py
@@ -565,7 +565,7 @@
     ua, ub, r1in, rr1, sa1, ra1, sb1, rb1, sc1, rc1, s1, r1, sq1, rq1, e2, cres, cq, cnew,
     p_ref, dir_ref, q_ref, r_ref,
     msg, gath, early, egath, wmsg, wgath, hb, he, sh, enmsg, engath, outs, back,
-    d_ssem, d_rsem, g_ssem, g_rsem, h_ssem, h_rsem, b_ssem, b_rsem, counted,
+    d_ssem, d_rsem, g_ssem, g_rsem, h_ssem, h_rsem, b_ssem, b_rsem, counted, columns,
 ):
     X, Y, Z = sizes
     nx, ny, nz = counts
@@ -1262,7 +1262,6 @@
         ends = jnp.where(y_at == GY - 1, 1.0, 0.0) + jnp.where(slab * S + row(S) == NZ - 1, 1.0, 0.0)
         ends_x = ends + jnp.where(x_last, 1.0, 0.0)
         fetch = lax.rem(lane_1, GY)
-        packed = jnp.zeros((1, LANES), f32)
         for k in range(TRIALS):
             s = jnp.exp2(-jnp.full((1, LANES), tp_ref[k], jnp.int32).astype(f32))
 
@@ -1277,13 +1276,15 @@
                 e = e + energy(v - jnp.where(y_first, 0.0, roll(v, 1, 1)))
                 e = e + energy(v) * (ends_x if t == X - 1 else ends)
                 e = e + (0.5 * f_rea[t, HALO : HALO + S] * v - f_src[t, HALO : HALO + S]) * v
-                column = jnp.sum(e, axis=0, keepdims=True)
-                step = 1
-                while step < GY:
-                    column = pair(column, step)
-                    step *= 2
-                packed = packed + jnp.where(fetch == k * X + t, column, 0.0)
+                columns[k * X + t : k * X + t + 1] = jnp.sum(e, axis=0, keepdims=True)
                 below = v
+        over_y = columns[...]
+        step = 1
+        while step < GY:
+            over_y = pair(over_y, step)
+            step *= 2
+        chosen = lax.rem(lane(TRIALS * X), GY) == row(TRIALS * X)
+        packed = jnp.sum(jnp.where(chosen, over_y, 0.0), axis=0, keepdims=True)
         enmsg[...] = packed
         engath[slab] = packed
         for other in range(nx * ny * nz):
@@ -1379,7 +1380,7 @@
     scratch += [vm(4 * C_ROWS, LANES), vm(NS * 4 * C_ROWS, LANES)]
     scratch += [vm(2, 2, 2 * (X + T1), HALO, LANES)] * 2 + [vm(2, 4, T1, HALO, LANES)]
     scratch += [vm(1, LANES), vm(NS, 1, LANES), vm(2, P, S, LANES), vm(2, Z, LANES)]
-    scratch += [sem(2, BLOCK + 2), sem(2, 3), sem(6), sem(6), sem(5, 2), sem(5, 2), sem(2), sem(2), vm(nx * ny * nz, 1, LANES)]
+    scratch += [sem(2, BLOCK + 2), sem(2, 3), sem(6), sem(6), sem(5, 2), sem(5, 2), sem(2), sem(2), vm(nx * ny * nz, 1, LANES), vm(TRIALS * X, LANES)]
     whole = pl.BlockSpec(memory_space=pltpu.VMEM)
     given = jnp.concatenate([v.reshape(LANES, Z) for v in (iterate, reaction, source)])
     fields, sums = pl.pallas_call(

time: 57.1 us -> 57.1 us (level)
  no operation moved by 1% of the time
where the time goes in v5:
time: 57.1 us; the launch traced here: 56.9 us
  Pallas kernels  55.3 us (97%)
  other arithmetic  0.92 us (2%)
  between operations  0.66 us (1%)
    pallas_call x1, Pallas kernels, slab_on_device(): pl.pallas_call(functools.partial(slab_kernel, (X, Y, Z), counts), out_sha...  54.6 us

profile of v5, /device:TPU:0, one launch (start us, length us, event | category | flops | bytes accessed | tf_op | source)
XLA Modules:
  0.0 56.9 jit_solution(8995898950332613070)
XLA Ops:
  0.6 0.0 copy-start
  0.6 0.9 %pad_maximum_fusion.given = f32[384,128]{1,0:T(8,128)S(1)} fusion(f32[128,128]{1,0:T(8,128)} %bitcast.3, f32[128,128]{1,0:T(8,128)} %bitcast.4, f32[128,128]{1,0:T(8,128)} %bitcast.5), kind=kLoop, calls=%fused_computation | loop fusion | flops 98304 | bytes 393216 | tf_op jit(solution)/shard_map/concatenate | solution.py:1385
  1.6 0.0 copy-done
  1.6 54.6 %newton_step.1 = (f32[2,8,16,128]{3,2,1,0:T(8,128)S(1)}, f32[8,128]{1,0:T(8,128)S(1)}) custom-call(s32[4]{0:T(128)S(1)} %copy-done, f32[384,128]{1,0:T(8,128)S(1)} %pad_maximum_fusion.given), custom_call_target="tpu_custom_call" | custom-call | tf_op jit(solution)/shard_map/newton_step/pallas_call | solution.py:1386
  56.2 0.7 %hand_out.1 = (f32[8,16,128]{2,1,0:T(8,128)}, f32[8,16,128]{2,1,0:T(8,128)}, f32[4,8]{1,0:T(4,128)}, f32[4]{0:T(128)}) custom-call(f32[2,8,16,128]{3,2,1,0:T(8,128)S(1)} %get-tuple-element.6.fields, f32[8,128]{1,0:T(8,128)S(1)} %get-tuple-element.7.sums), custom_call_target="tpu_custom_call" | custom-call | tf_op jit(solution)/shard_map/hand_out/pallas_call | solution.py:1397
Async XLA Ops:
  0.6 0.9 %copy-start = (s32[4]{0:T(128)S(1)}, s32[4]{0:T(128)}, u32[]{:S(2)}) copy-start(s32[4]{0:T(128)} %tp_ref.1) | copy-start | bytes 52
